TPU v7x, 256 devices: a whole 4x4x8 slice. The times are simulated.
256 devices in a mesh: row: 32 (over x_hi, z, core), ga: 8 (over x_lo, y).
Axes of the slice: x: 4 (x_hi: 2, x_lo: 2; x = x_hi * 2 + x_lo), y: 4, z: 8, core: 2. Of those that a mesh axis runs over, the one named last changes fastest.
Arguments:
- pair_dens: bfloat16 [32, 256, 4096], P('row', None, 'ga'), may hold values from -0.41992188 to 0.41992188
- cond_dens: bfloat16 [32, 1024, 4096], P('row', None, 'ga'), may hold values from -0.41992188 to 0.41992188
- val_dens: bfloat16 [32, 64, 4096], P(None, None, 'row'), may hold values from -0.41992188 to 0.41992188
- screened: bfloat16 [8, 4096, 4096], P(None, 'ga', 'row'), may hold values from -1 to 6, as said below
- coulomb: bfloat16 [4096], P('ga'), may hold values from 0.29882812 to 10
- pair_list: int32 [32, 256], replicated, may hold values from 0 to 255, each once within a row
- counts: int32 [32], replicated, may hold values from 10 to 256
- q_index: int32 [32], replicated, may hold values from 0 to 7
- column_k: int32 [1], replicated, may hold values from 0 to 31
Outputs:
- kernel: bfloat16 [8192, 256], P('row', 'ga')
Inputs may be any that keep to these rules, and one draw needn't show every extreme that they name: `screened`: each diagonal entry exceeds the sum of the magnitudes of the others in its row divided by the square root of 4096 times four.
All inputs are finite; a program needn't handle non-finite values.
Results may differ from a plain program's by a relative error of at most 0.0042.
Values may be sent and summed in bfloat16 or wider, within the bound.
No kernel may reach another device: no remote copies, remote signals or barrier semaphores. Data moves between devices by JAX's collectives and lax.ppermute only.
A program may use at most 64 MiB of HBM per device.

v0:
```python
import jax
import jax.numpy as jnp
from jax import lax
from jax.sharding import PartitionSpec as P

NV = 8
NC = 32


def picked(shard, axis, root):
    return lax.dynamic_index_in_dim(lax.all_gather(shard, axis), root, 0, keepdims=False)


def split_up(shard, dim, devices):
    lengths = shard.shape
    parts = shard.reshape(*lengths[:dim], devices, lengths[dim] // devices, *lengths[dim + 1 :])
    return jnp.moveaxis(parts, dim, 0)


def sum_at_owner(shard, axis, dim):
    devices = lax.axis_size(axis)
    parts = lax.all_to_all(split_up(shard, dim, devices), axis, 0, 0, tiled=True)
    return jnp.sum(parts.astype(jnp.float32), axis=0)


def sum_at_owner_2(shard, axis, dim):
    parts = split_up(shard, dim, lax.axis_size(axis))
    arrived = lax.all_to_all(parts, axis, split_axis=0, concat_axis=0, tiled=True)
    return arrived.sum(axis=0)


def per_device(
    pair_dens, cond_dens, val_dens, screened, coulomb, pair_list, counts, q_index, column_k
):
    kdev = pair_dens.shape[0]
    slots_all = pair_dens.shape[1]
    mine = lax.axis_index("row")
    column = column_k[0]
    root = column // kdev
    local_slot = column % kdev
    own_col = lax.dynamic_index_in_dim(pair_dens, local_slot, 0, keepdims=False)
    col_full = picked(own_col, "row", root)
    col_pairs = pair_list[column]
    col = jnp.take(col_full, col_pairs, axis=0)
    first = mine * kdev
    my_pairs = lax.dynamic_slice_in_dim(pair_list, first, kdev, 0)
    my_counts = lax.dynamic_slice_in_dim(counts, first, kdev, 0)
    blocks = jnp.take(screened, q_index, axis=0)
    screened_val = sum_at_owner(
        jnp.einsum("kvg,khg->kvh", val_dens, blocks, preferred_element_type=jnp.float32).astype(
            jnp.bfloat16
        ),
        "row",
        0,
    )
    screened_val = screened_val.astype(jnp.bfloat16)
    direct_full = jnp.einsum(
        "kag,kvg->kav", cond_dens, screened_val, preferred_element_type=jnp.float32
    )
    arranged = (
        direct_full.reshape(kdev, NC, NC, NV, NV)
        .transpose(0, 3, 1, 4, 2)
        .reshape(kdev, slots_all, slots_all)
    )
    direct = jnp.take(
        jnp.take_along_axis(arranged, my_pairs[:, :, None], axis=1), col_pairs, axis=2
    )
    rows = jnp.take_along_axis(pair_dens, my_pairs[:, :, None], axis=1)
    weighted = (rows.astype(jnp.float32) * coulomb.astype(jnp.float32)[None, None, :]).astype(
        jnp.bfloat16
    )
    exch = jnp.einsum("ksg,tg->kst", weighted, col, preferred_element_type=jnp.float32)
    slot_ids = jnp.arange(slots_all, dtype=jnp.int32)
    row_mask = (slot_ids[None, :] < my_counts[:, None]).astype(jnp.float32)
    col_mask = (slot_ids < counts[column]).astype(jnp.float32)
    masking = row_mask[:, :, None] * col_mask[None, None, :]
    combined = ((2.0 * exch - direct) * masking).reshape(kdev * slots_all, slots_all)
    summed = sum_at_owner_2(combined, "ga", 1)
    return summed.astype(jnp.bfloat16)


def solution(mesh):
    placed = (
        P("row", None, "ga"),
        P("row", None, "ga"),
        P(None, None, "row"),
        P(None, "ga", "row"),
        P("ga"),
        P(),
        P(),
        P(),
        P(),
    )
    return jax.shard_map(
        per_device, mesh=mesh, in_specs=placed, out_specs=P("row", "ga"), check_vma=False
    )
```

profile of v0, /device:TPU:2, one launch (start us, length us, event | category | flops | bytes accessed | tf_op | source)
XLA Modules:
  0.0 152.4 jit_solution(6338403845606772508)
XLA Ops:
  6.5 0.0 copy-start
  6.5 0.0 all-gather.2.cloned.1.call-start
  6.5 0.7 all-gather.2.cloned.1.call-update
  7.3 0.7 compare_select_fusion.4
  7.9 0.0 copy-done
  7.9 0.0 copy-start.6
  7.9 0.0 copy-start.5
  8.0 3.1 %gather_fusion.2 = bf16[32,512,128]{2,1,0:T(8,128)(2,1)} fusion(bf16[8,512,128]{2,1,0:T(8,128)(2,1)S(1)} %copy-done, s32[1024]{0:T(1024)S(1)} %pad_clamp_fusion), kind=kCustom, calls=%fused_computation.2 | custom fusion | bytes 8388736 | tf_op jit(solution)/shard_map/jit(_take)/gather | solution.py:48
  11.0 0.0 copy-done.6
  11.0 0.0 copy-done.5
  11.0 0.0 copy-start.4
  11.0 0.0 copy-start.1
  11.1 5.2 %convert_bitcast_fusion = bf16[32,1,64,512]{3,2,1,0:T(8,128)(2,1)} fusion(bf16[32,64,128]{2,1,0:T(8,128)(2,1)S(1)} %copy-done.5, bf16[32,512,128]{2,1,0:T(8,128)(2,1)} %gather_fusion.2, pred[32]{0:T(512)(128)(4,1)S(1)} %compare_and_fusion), kind=kOutput, calls=%fused_computation.8 | convolution fusion | flops 271581184 | bytes 6815776 | tf_op jit(solution)/shard_map/kvg,khg->kvh/dot_general | solution.py:50
  16.3 0.0 copy-start.3
  16.3 10.5 %all-to-all-start = ((bf16[32,1,64,512]{3,2,1,0:T(8,128)(2,1)}), bf16[32,1,64,512]{3,2,1,0:T(8,128)(2,1)S(1)}, u32[]{:S(2)}, u32[]{:S(2)}) async-start(bf16[32,1,64,512]{3,2,1,0:T(8,128)(2,1)} %convert_bitcast_fusion), calls=%async_computation | async-start | bytes 4194304 | tf_op jit(solution)/shard_map/all_to_all | solution.py:22
  27.5 0.0 copy-done.4
  27.5 0.7 compare_select_fusion
  28.3 0.0 copy-done.1
  28.3 1.9 %gather_fusion = bf16[256,512]{1,0:T(8,128)(2,1)} fusion(bf16[256,512]{1,0:T(8,128)(2,1)S(1)} %bitcast.54, s32[1024]{0:T(1024)S(1)} %pad_clamp_fusion.2), kind=kCustom, calls=%fused_computation | custom fusion | bytes 525312 | tf_op jit(solution)/shard_map/jit(take_along_axis)/gather | solution.py:68
  30.2 0.0 copy-done.3
  30.2 0.7 fusion.18
  30.8 1.3 compare_convert_fusion
  32.2 55.5 %all-to-all-done = bf16[32,1,64,512]{3,2,1,0:T(8,128)(2,1)S(1)} async-done(((bf16[32,1,64,512]{3,2,1,0:T(8,128)(2,1)}), bf16[32,1,64,512]{3,2,1,0:T(8,128)(2,1)S(1)}, u32[]{:S(2)}, u32[]{:S(2)}) %all-to-all-start) | async-done | bytes 2097184 | tf_op jit(solution)/shard_map/all_to_all | solution.py:22
  87.7 0.3 reduce_sum.21
  88.0 2.2 %convolution_bitcast_fusion = f32[1,8,32,8,32]{4,3,2,1,0:T(8,128)S(1)} fusion(bf16[32,32,512,1]{2,1,0,3:T(8,128)(2,1)} %bitcast.55, bf16[64,512]{1,0:T(8,128)(2,1)S(1)} %reduce_sum.21), kind=kOutput, calls=%fused_computation.10 | convolution fusion | flops 67108864 | bytes 1376256 | tf_op jit(solution)/shard_map/kag,kvg->kav/dot_general | solution.py:57
  90.2 0.3 reshape.233
  90.5 0.0 copy-start.2
  90.5 1.0 gather_fusion.3
  91.5 0.1 fusion.8
  91.6 0.1 copy.13
  91.7 1.0 gather_fusion.4
  92.7 37.8 %all-gather.2.cloned.1.call-done = bf16[32,256,512]{2,1,0:T(8,128)(2,1)} async-done(((bf16[1,256,512]{2,1,0:T(8,128)(2,1)}), bf16[32,256,512]{2,1,0:T(8,128)(2,1)}) %all-gather.2.cloned.1.call-update) | async-done | bytes 8388624 | tf_op jit(solution)/shard_map/all_gather | solution.py:11
  130.5 1.0 dynamic-slice_bitcast_fusion
  131.5 1.2 gather_fusion.1
  132.6 0.0 copy-done.2
  132.6 0.4 fusion.7
  133.0 11.9 %all_to_all.10 = f32[8,256,32]{1,2,0:T(8,128)S(1)} all-to-all(f32[8,256,32]{1,2,0:T(8,128)S(1)} %bitcast.56), channel_id=1, replica_groups=mesh['row'=32,'ga'=8] {'ga'}, dimensions={0} | all-to-all | bytes 524288 | tf_op jit(solution)/shard_map/all_to_all | solution.py:28
  144.9 0.6 reduce_sum.22
  (6 shorter events, 0.0 us)
Async XLA Ops:
  6.5 1.4 copy-start
  6.5 124.0 %all-gather.2.cloned.1.call-start = ((), (), s32[]{:S(2)}) async-start(), calls=%async_computation.2 | async-start | bytes 8650752 | tf_op jit(solution)/shard_map/all_gather | solution.py:11
  7.9 3.1 %copy-start.6 = (s32[32]{0:T(128)S(1)}, s32[32]{0:T(128)}, u32[]{:S(2)}) copy-start(s32[32]{0:T(128)} %param.16) | copy-start | bytes 388
  7.9 3.1 %copy-start.5 = (bf16[32,64,128]{2,1,0:T(8,128)(2,1)S(1)}, bf16[32,64,128]{2,1,0:T(8,128)(2,1)}, u32[]{:S(2)}) copy-start(bf16[32,64,128]{2,1,0:T(8,128)(2,1)} %param.11) | copy-start | bytes 1572868
  11.0 16.5 %copy-start.4 = (bf16[512]{0:T(512)(128)(2,1)S(1)}, bf16[512]{0:T(512)(128)(2,1)}, u32[]{:S(2)}) copy-start(bf16[512]{0:T(512)(128)(2,1)} %param.13) | copy-start | bytes 3076
  11.0 17.2 %copy-start.1 = (bf16[1,256,512]{2,1,0:T(8,128)(2,1)S(1)}, bf16[1,256,512]{2,1,0:T(8,128)(2,1)}, u32[]{:S(2)}) copy-start(bf16[1,256,512]{2,1,0:T(8,128)(2,1)} %param.9) | copy-start | bytes 786436
  16.3 13.9 %copy-start.3 = (s32[32]{0:T(128)S(1)}, s32[32]{0:T(128)}, u32[]{:S(2)}) copy-start(s32[32]{0:T(128)} %param.15) | copy-start | bytes 388
  16.3 71.4 %all-to-all-start = ((bf16[32,1,64,512]{3,2,1,0:T(8,128)(2,1)}), bf16[32,1,64,512]{3,2,1,0:T(8,128)(2,1)S(1)}, u32[]{:S(2)}, u32[]{:S(2)}) async-start(bf16[32,1,64,512]{3,2,1,0:T(8,128)(2,1)} %convert_bitcast_fusion), calls=%async_computation | async-start | bytes 4194304 | tf_op jit(solution)/shard_map/all_to_all | solution.py:22
  90.5 42.1 %copy-start.2 = (bf16[256,512]{1,0:T(8,128)(2,1)S(1)}, bf16[256,512]{1,0:T(8,128)(2,1)}, u32[]{:S(2)}) copy-start(bf16[256,512]{1,0:T(8,128)(2,1)} %gather_fusion) | copy-start | bytes 786436
Sparse Core Ops, SparseCore 0:
  10.1 120.3 all-gather.1
where the time goes:
time: 153 us; the launch traced here: 152 us
  waiting for transfers between devices  94 us (61%)
  between operations  14.2 us (9%)
  blocking collectives  11.9 us (8%)
  starting transfers between devices  10.6 us (7%)
  local copies, waits for them, and re-layouts  10.2 us (7%)
  matrix products  7.76 us (5%)
  other arithmetic  3.79 us (2%)
    all_to_all x1, waiting for transfers between devices, sum_at_owner(): lax.all_to_all(split_up(shard, dim, devices), axis, 0, 0, tiled=True)  55.5 us
    all_gather x1, waiting for transfers between devices, picked(): lax.all_gather(shard, axis)  37.8 us
    all_to_all x1, blocking collectives, sum_at_owner_2(): lax.all_to_all(parts, axis, split_axis=0, concat_axis=0, tiled=True)  11.9 us
    all_to_all x1, starting transfers between devices, sum_at_owner(): lax.all_to_all(split_up(shard, dim, devices), axis, 0, 0, tiled=True)  10.5 us
    dot_general x1, matrix products, per_device(): jnp.einsum('kvg,khg->kvh', val_dens, blocks, preferred_element_type=jnp.f...  5.22 us
  transfers between devices with their start and end apart: 2, of which 2 were waited for; matrix products, arithmetic and copies ran while one was open for 12% of the time, Pallas kernels for 0%

commit v1 on v0

v1 whole, which is shorter than its diff:
```python
import jax
import jax.numpy as jnp
from jax import lax
from jax.experimental import pallas as pl
from jax.experimental.pallas import tpu as pltpu
from jax.sharding import Mesh
from jax.sharding import PartitionSpec as P

NV = 8
NC = 32
XH, Z, CORE, XL, Y = 2, 8, 2, 2, 4
ROW = ("xh", "z", "core")
GA = ("xl", "y")
BF = jnp.bfloat16
F32 = jnp.float32
VMEM = pl.BlockSpec(memory_space=pltpu.VMEM)
SMEM = pl.BlockSpec(memory_space=pltpu.SMEM)
LAST = (((1,), (1,)), ((), ()))


def call(body, out, specs, flops=1 << 20, nbytes=1 << 20):
    many = isinstance(out, (list, tuple))
    return pl.pallas_call(
        body,
        out_shape=out,
        in_specs=specs,
        out_specs=tuple(VMEM for _ in out) if many else VMEM,
        cost_estimate=pl.CostEstimate(flops=flops, bytes_accessed=nbytes, transcendentals=0),
    )


def shaped(shape, dtype):
    return jax.ShapeDtypeStruct(shape, dtype)


def dot(a, b):
    return lax.dot_general(a, b, LAST, preferred_element_type=F32)


def partial_sums(other_x, other_core, q_index, val, screened, added, dtype):
    planes, vv, hh = Z, val.shape[1], screened.shape[1]

    def body(q_ref, val_ref, w_ref, *refs):
        out_ref = refs[-1]
        xh, core = lax.axis_index("xh"), lax.axis_index("core")
        xh = 1 - xh if other_x else xh
        core = 1 - core if other_core else core
        for z in range(planes):
            k = (xh * Z + z) * CORE + core
            r = dot(val_ref[k], w_ref[q_ref[k]])
            if len(refs) == 2:
                r = r + refs[0][z].astype(F32)
            out_ref[z] = r.astype(dtype)

    args = (q_index, val, screened) + (() if added is None else (added,))
    specs = [SMEM, VMEM, VMEM] + ([] if added is None else [VMEM])
    flops = 2 * planes * vv * hh * val.shape[2]
    return call(body, shaped((planes, vv, hh), dtype), specs, flops, 2 << 20)(*args)


def half_of_column(column, own, sib):
    half = own.shape[1] // 2

    def body(c_ref, own_ref, sib_ref, out_ref):
        core = lax.axis_index("core")
        rows = pl.ds(pl.multiple_of(core * half, half), half)
        mine = c_ref[0] % CORE == core

        @pl.when(mine)
        def _():
            out_ref[...] = own_ref[0, rows, :]

        @pl.when(jnp.logical_not(mine))
        def _():
            out_ref[...] = sib_ref[0, rows, :]

    return call(body, shaped((half, own.shape[2]), BF), [SMEM, VMEM, VMEM])(column, own, sib)


def piece_for_all(column, parts):
    def body(c_ref, in_ref, out_ref):
        z = (c_ref[0] // CORE) % Z
        piece = in_ref[z]
        for i in range(Z):
            out_ref[i] = piece

    return call(body, shaped(parts.shape, BF), [SMEM, VMEM])(column, parts)


def exchange_terms(column, counts, pair_list, pair_dens, coulomb, halves):
    slots, g = pair_dens.shape[1:]
    half = slots // 2

    def body(c_ref, n_ref, pl_ref, pd_ref, cou_ref, own_ref, sib_ref, ox_ref, sx_ref, ex_ref, pt_ref, ps_ref, col_ref):
        xh, z, core = (lax.axis_index(a) for a in ROW)
        k = (xh * Z + z) * CORE + core
        ck = c_ref[0]
        same = ck // (Z * CORE) == xh
        first = pl.ds(pl.multiple_of(core * half, half), half)
        second = pl.ds(pl.multiple_of((1 - core) * half, half), half)

        @pl.when(same)
        def _():
            col_ref[first, :] = own_ref[...]
            col_ref[second, :] = sib_ref[...]

        @pl.when(jnp.logical_not(same))
        def _():
            col_ref[first, :] = ox_ref[...]
            col_ref[second, :] = sx_ref[...]

        weighted = (pd_ref[0].astype(F32) * cou_ref[...].astype(F32)).astype(BF)
        ex_ref[...] = 2.0 * dot(col_ref[...], weighted)
        pair = lax.broadcasted_iota(jnp.int32, (slots, slots), 0)
        slot = lax.broadcasted_iota(jnp.int32, (slots, slots), 1)
        mine = (pair == pl_ref[pl.ds(k, 1), :]) & (slot < n_ref[k])
        ps_ref[...] = mine.astype(F32).astype(BF)
        theirs = (pair == pl_ref[pl.ds(ck, 1), :]) & (slot < n_ref[ck])
        pt_ref[...] = theirs.astype(F32).T.astype(BF)

    square = (slots, slots)
    return pl.pallas_call(
        body,
        out_shape=(shaped(square, F32), shaped(square, BF), shaped(square, BF)),
        in_specs=[SMEM, SMEM] + [VMEM] * 7,
        out_specs=(VMEM, VMEM, VMEM),
        scratch_shapes=[pltpu.VMEM((slots, g), BF)],
        cost_estimate=pl.CostEstimate(flops=2 * slots * slots * g, bytes_accessed=1 << 20, transcendentals=0),
    )(column, counts, pair_list, pair_dens, coulomb.reshape(1, g), *halves)


def combine(arrived, cond_t, ex2, pt):
    slots = ex2.shape[0]
    vv, hh = arrived.shape[1:]

    def body(y_ref, cond_ref, ex_ref, pt_ref, out_ref, s_ref):
        sv = jnp.sum(y_ref[...].astype(F32), axis=0).astype(BF)
        r = dot(sv, cond_ref[...])
        for c in range(NC):
            s_ref[pl.ds(c, vv, stride=NC), :] = r[:, c * NC : (c + 1) * NC]
        direct = jnp.concatenate([s_ref[v * slots : (v + 1) * slots, :] for v in range(NV)], axis=1)
        terms = (ex_ref[...] - direct).astype(BF)
        out_ref[...] = jnp.dot(pt_ref[...], terms, preferred_element_type=F32).astype(BF)

    return pl.pallas_call(
        body,
        out_shape=shaped((slots, slots), BF),
        in_specs=[VMEM] * 4,
        out_specs=VMEM,
        scratch_shapes=[pltpu.VMEM((vv * NC, NC), F32)],
        cost_estimate=pl.CostEstimate(flops=2 * vv * NC * NC * hh, bytes_accessed=2 << 20, transcendentals=0),
    )(arrived, cond_t, ex2, pt)


def finish(parts, ps):
    def body(in_ref, ps_ref, out_ref):
        total = jnp.sum(in_ref[...].astype(F32), axis=0).astype(BF)
        out_ref[...] = jnp.dot(total, ps_ref[...], preferred_element_type=F32).astype(BF)

    return call(body, shaped(parts.shape[1:], BF), [VMEM, VMEM])(parts, ps)


def swap(x, axis):
    return lax.ppermute(x, axis, [(0, 1), (1, 0)])


def per_device(
    pair_dens, cond_dens, val_dens, screened, coulomb, pair_list, counts, q_index, column_k
):
    slots, g = pair_dens.shape[1:]
    terms = lambda ox, oc, added, dtype: partial_sums(ox, oc, q_index, val_dens, screened, added, dtype)
    to_core = swap(terms(True, True, None, BF), "core")
    sib = swap(pair_dens, "core")
    to_x = terms(True, False, to_core, BF)
    from_x = swap(to_x, "xh")
    to_core_2 = swap(terms(False, True, None, BF), "core")
    own = terms(False, False, to_core_2, F32)
    half = half_of_column(column_k, pair_dens, sib)
    parts = lax.all_to_all(half.reshape(Z, -1, g), "z", 0, 0, tiled=True)
    spread = lax.all_to_all(piece_for_all(column_k, parts), "z", 0, 0, tiled=True)
    own_half = spread.reshape(half.shape)
    sib_half = swap(own_half, "core")
    own_half_x = swap(own_half, "xh")
    sib_half_x = swap(sib_half, "xh")
    to_z = (own + from_x.astype(F32)).astype(BF)
    arrived = lax.all_to_all(to_z, "z", 0, 0, tiled=True)
    ex2, pt, ps = exchange_terms(
        column_k, counts, pair_list, pair_dens, coulomb, (own_half, sib_half, own_half_x, sib_half_x)
    )
    cond_t = cond_dens.reshape(NC, NC, g).transpose(1, 0, 2).reshape(NC * NC, g)
    combined = combine(arrived, cond_t, ex2, pt)
    blocks = lax.all_to_all(combined.reshape(XL * Y, -1, slots), GA, 0, 0, tiled=True)
    return finish(blocks, ps).T


def solution(mesh):
    fine = Mesh(mesh.devices.reshape(XH, Z, CORE, XL, Y), ROW + GA)
    placed = (
        P(ROW, None, GA),
        P(ROW, None, GA),
        P(None, None, ROW),
        P(None, GA, ROW),
        P(GA),
        P(),
        P(),
        P(),
        P(),
    )
    return jax.shard_map(
        per_device, mesh=fine, in_specs=placed, out_specs=P(ROW, GA), check_vma=False
    )
```

time: 153 us -> 85.5 us (0.56)
  waiting for transfers between devices: 94 us -> 10.8 us
  Pallas kernels: 0 us -> 21.9 us
  blocking collectives: 11.9 us -> 29.2 us
  between operations: 14.2 us -> 0.72 us
  matrix products: 7.76 us -> 0 us
  local copies, waits for them, and re-layouts: 10.2 us -> 5.92 us
  starting transfers between devices: 10.6 us -> 14 us
  other arithmetic: 3.79 us -> 2.18 us
    all_to_all x1 -> x2, waiting for transfers between devices: 55.5 us -> 5.52 us  [the longest x1 2.96 us: per_device(): lax.all_to_all(piece_for_all(column_k, parts), 'z', 0, 0, tiled=True)]
    all_gather x1 -> x0, waiting for transfers between devices: 37.8 us -> none  [picked(): lax.all_gather(shard, axis)]
    pallas_call x0 -> x9, Pallas kernels: none -> 21.9 us  [the longest x4 11.2 us: partial_sums(): call(body, shaped((planes, vv, hh), dtype), specs, flops, 2 << 20)(*args)]
    all_to_all x1 -> x2, blocking collectives: 11.9 us -> 29.2 us  [the longest x1 17.9 us: per_device(): parts = lax.all_to_all(half.reshape(Z, -1, g), 'z', 0, 0, tiled=True)]
    gather x5 -> x0, local copies, waits for them, and re-layouts: 8.04 us -> none  [the longest x1 3.05 us: per_device(): blocks = jnp.take(screened, q_index, axis=0)]
    dot_general x3 -> x0, matrix products: 7.76 us -> none  [the longest x1 5.22 us: per_device(): jnp.einsum('kvg,khg->kvh', val_dens, blocks, preferred_element_type=jnp.f...]
    ppermute x0 -> x7, starting transfers between devices: none -> 6.33 us  [swap(): return lax.ppermute(x, axis, [(0, 1), (1, 0)])]
    ppermute x0 -> x7, waiting for transfers between devices: none -> 5.3 us  [swap(): return lax.ppermute(x, axis, [(0, 1), (1, 0)])]
  transfers between devices with their start and end apart: 2 -> 9, of which waited for: 2 -> 5; matrix products, arithmetic and copies ran while one was open for 12% -> 5% of each run, Pallas kernels for 0% -> 17%
where the time goes in v1:
time: 85.5 us; the launch traced here: 84.8 us
  blocking collectives  29.2 us (34%)
  Pallas kernels  21.9 us (26%)
  starting transfers between devices  14 us (16%)
  waiting for transfers between devices  10.8 us (13%)
  local copies, waits for them, and re-layouts  5.92 us (7%)
  other arithmetic  2.18 us (3%)
    all_to_all x1, blocking collectives, per_device(): parts = lax.all_to_all(half.reshape(Z, -1, g), 'z', 0, 0, tiled=True)  17.9 us
    all_to_all x1, blocking collectives, per_device(): lax.all_to_all(combined.reshape(XL * Y, -1, slots), GA, 0, 0, tiled=True)  11.3 us
    pallas_call x4, Pallas kernels, partial_sums(): call(body, shaped((planes, vv, hh), dtype), specs, flops, 2 << 20)(*args)  11.2 us
    ppermute x7, starting transfers between devices, swap(): return lax.ppermute(x, axis, [(0, 1), (1, 0)])  6.33 us
    ppermute x7, waiting for transfers between devices, swap(): return lax.ppermute(x, axis, [(0, 1), (1, 0)])  5.3 us
    all_to_all x1, starting transfers between devices, per_device(): arrived = lax.all_to_all(to_z, 'z', 0, 0, tiled=True)  4.29 us
    unnamed x22, local copies, waits for them, and re-layouts  3.76 us
    pallas_call x1, Pallas kernels, combine(): pl.pallas_call(body, out_shape=shaped((slots, slots), BF), in_specs=[VMEM...  3.48 us
  transfers between devices with their start and end apart: 9, of which 5 were waited for; matrix products, arithmetic and copies ran while one was open for 5% of the time, Pallas kernels for 17%

profile of v1, /device:TPU:2, one launch (start us, length us, event | category | flops | bytes accessed | tf_op | source)
XLA Modules:
  0.0 84.8 jit_solution(1373892320482036012)
XLA Ops:
  0.0 2.7 %shard_map.93 = bf16[8,64,512]{2,1,0:T(8,128)(2,1)} custom-call(s32[32]{0:T(128)} %q_ref.7, bf16[32,64,128]{2,1,0:T(8,128)(2,1)} %val_ref.7, bf16[8,512,128]{2,1,0:T(8,128)(2,1)} %w_ref.7), custom_call_target="tpu_custom_call" | custom-call | flops 67108864 | bytes 2097152 | tf_op jit(solution)/shard_map/pallas_call | solution.py:58
  2.7 0.0 collective-permute-start.1
  2.7 2.7 %shard_map.91 = bf16[8,64,512]{2,1,0:T(8,128)(2,1)} custom-call(s32[32]{0:T(128)} %q_ref.7, bf16[32,64,128]{2,1,0:T(8,128)(2,1)} %val_ref.7, bf16[8,512,128]{2,1,0:T(8,128)(2,1)} %w_ref.7), custom_call_target="tpu_custom_call" | custom-call | flops 67108864 | bytes 2097152 | tf_op jit(solution)/shard_map/pallas_call | solution.py:58
  5.4 0.0 copy-start.2
  5.4 0.5 collective-permute-start
  5.9 0.0 collective-permute-done.1.refs_0_
  5.9 0.0 copy-start.5
  5.9 0.8 copy-done.5
  6.7 2.8 %shard_map.94 = bf16[8,64,512]{2,1,0:T(8,128)(2,1)} custom-call(s32[32]{0:T(128)} %q_ref.7, bf16[32,64,128]{2,1,0:T(8,128)(2,1)} %val_ref.7, bf16[8,512,128]{2,1,0:T(8,128)(2,1)} %w_ref.7, bf16[8,64,512]{2,1,0:T(8,128)(2,1)} %copy-done.5), custom_call_target="tpu_custom_call" | custom-call | flops 67108864 | bytes 2097152 | tf_op jit(solution)/shard_map/pallas_call | solution.py:58
  9.5 2.1 %collective-permute-start.2 = (bf16[8,64,512]{2,1,0:T(8,128)(2,1)}, bf16[8,64,512]{2,1,0:T(8,128)(2,1)S(1)}, u32[]{:S(2)}, u32[]{:S(2)}) collective-permute-start(bf16[8,64,512]{2,1,0:T(8,128)(2,1)} %shard_map.94), channel_id=1, source_target_pairs={{0,128},{128,0},{1,129},{129,1},{2,130},{130,2},{3,131},{131,3},{4... | collective-permute-start | bytes 1572872 | tf_op jit(solution)/shard_map/ppermute | solution.py:164
  11.6 0.0 copy-done.2
  11.7 0.0 collective-permute-start.3
  12.3 0.9 %collective-permute-done.3.sib_ref = bf16[1,256,512]{2,1,0:T(8,128)(2,1)S(1)} collective-permute-done((bf16[1,256,512]{2,1,0:T(8,128)(2,1)S(1)}, bf16[1,256,512]{2,1,0:T(8,128)(2,1)S(1)}, u32[]{:S(2)}, u32[]{:S(2)}) %collective-permute-start.3) | collective-permute-done | bytes 262176 | tf_op jit(solution)/shard_map/ppermute | solution.py:164
  13.2 0.0 copy-start.6
  13.2 0.7 copy-done.6
  13.9 1.7 %shard_map.95 = bf16[128,512]{1,0:T(8,128)(2,1)} custom-call(s32[1]{0:T(128)S(6)} %copy.11.c_ref, bf16[1,256,512]{2,1,0:T(8,128)(2,1)} %pd_ref.1, bf16[1,256,512]{2,1,0:T(8,128)(2,1)} %copy-done.6), custom_call_target="tpu_custom_call" | custom-call | flops 1048576 | bytes 1048576 | tf_op jit(solution)/shard_map/pallas_call | solution.py:77
  15.6 17.9 %all_to_all.20.in_ref = bf16[8,16,512]{2,1,0:T(8,128)(2,1)} all-to-all(bf16[8,16,512]{2,1,0:T(8,128)(2,1)} %bitcast.14), channel_id=1, replica_groups=mesh['xh'=2,'z'=8,'core'=2,'xl'=2,'y'=4] {'z'}, dimensions={0} | all-to-all | bytes 262144 | tf_op jit(solution)/shard_map/all_to_all | solution.py:179
  33.5 1.6 %shard_map.96 = bf16[8,16,512]{2,1,0:T(8,128)(2,1)} custom-call(s32[1]{0:T(128)S(6)} %copy.11.c_ref, bf16[8,16,512]{2,1,0:T(8,128)(2,1)} %all_to_all.20.in_ref), custom_call_target="tpu_custom_call" | custom-call | flops 1048576 | bytes 1048576 | tf_op jit(solution)/shard_map/pallas_call | solution.py:87
  35.1 3.4 %all-to-all-start.2 = ((bf16[8,16,512]{2,1,0:T(8,128)(2,1)}), bf16[8,16,512]{2,1,0:T(8,128)(2,1)S(1)}, u32[]{:S(2)}, u32[]{:S(2)}) async-start(bf16[8,16,512]{2,1,0:T(8,128)(2,1)} %shard_map.96), calls=%async_computation.2 | async-start | bytes 262144 | tf_op jit(solution)/shard_map/all_to_all | solution.py:180
  38.5 0.0 collective-permute-done.refs_0_
  38.5 0.0 copy-start.4
  38.5 0.8 copy-done.4
  39.3 3.0 %shard_map.92 = f32[8,64,512]{2,1,0:T(8,128)} custom-call(s32[32]{0:T(128)} %q_ref.7, bf16[32,64,128]{2,1,0:T(8,128)(2,1)} %val_ref.7, bf16[8,512,128]{2,1,0:T(8,128)(2,1)} %w_ref.7, bf16[8,64,512]{2,1,0:T(8,128)(2,1)} %copy-done.4), custom_call_target="tpu_custom_call" | custom-call | flops 67108864 | bytes 2097152 | tf_op jit(solution)/shard_map/pallas_call | solution.py:58
  42.3 0.0 collective-permute-done.2
  42.3 2.2 %add_convert_fusion = bf16[8,64,512]{2,1,0:T(8,128)(2,1)} fusion(f32[8,64,512]{2,1,0:T(8,128)} %shard_map.92, bf16[8,64,512]{2,1,0:T(8,128)(2,1)S(1)} %collective-permute-done.2), kind=kLoop, calls=%fused_computation | loop fusion | flops 786432 | bytes 2097152 | tf_op jit(solution)/shard_map/convert_element_type | solution.py:185
  44.5 0.0 copy-start.1
  44.5 3.0 %all-to-all-done.2 = bf16[8,16,512]{2,1,0:T(8,128)(2,1)S(1)} async-done(((bf16[8,16,512]{2,1,0:T(8,128)(2,1)}), bf16[8,16,512]{2,1,0:T(8,128)(2,1)S(1)}, u32[]{:S(2)}, u32[]{:S(2)}) %all-to-all-start.2) | async-done | bytes 131104 | tf_op jit(solution)/shard_map/all_to_all | solution.py:180
  47.5 4.3 %all-to-all-start = ((bf16[8,64,512]{2,1,0:T(8,128)(2,1)}), bf16[8,64,512]{2,1,0:T(8,128)(2,1)S(1)}, u32[]{:S(2)}, u32[]{:S(2)}) async-start(bf16[8,64,512]{2,1,0:T(8,128)(2,1)} %add_convert_fusion), calls=%async_computation | async-start | bytes 1048576 | tf_op jit(solution)/shard_map/all_to_all | solution.py:186
  51.8 0.1 collective-permute-start.4
  51.9 0.0 copy-done.3
  51.9 1.5 %collective-permute-start.5 = (bf16[128,512]{1,0:T(8,128)(2,1)S(1)}, bf16[128,512]{1,0:T(8,128)(2,1)S(1)}, u32[]{:S(2)}, u32[]{:S(2)}) collective-permute-start(bf16[128,512]{1,0:T(8,128)(2,1)S(1)} %bitcast.11), channel_id=1, source_target_pairs={{0,128},{128,0},{1,129},{129,1},{2,130},{130,2},{3,131},{131,3},{4... | collective-permute-start | bytes 393224 | tf_op jit(solution)/shard_map/ppermute | solution.py:164
  53.4 0.0 collective-permute-done.4.sib_ref
  53.4 2.1 %collective-permute-start.6 = (bf16[128,512]{1,0:T(8,128)(2,1)S(1)}, bf16[128,512]{1,0:T(8,128)(2,1)S(1)}, u32[]{:S(2)}, u32[]{:S(2)}) collective-permute-start(bf16[128,512]{1,0:T(8,128)(2,1)S(1)} %collective-permute-done.4.sib_ref), channel_id=1, source_target_pairs={{0,128},{128,0},{1,129},{129,1},{2,130},{130,2},{3,131},{131,3},{4... | collective-permute-start | bytes 393224 | tf_op jit(solution)/shard_map/ppermute | solution.py:164
  55.5 0.0 copy-done.10
  55.5 0.6 reshape.20.cou_ref
  56.1 0.0 copy-done.1
  56.1 1.6 %copy.10 = bf16[32,32,512]{2,0,1:T(8,128)(2,1)} copy(bf16[32,32,512]{2,1,0:T(8,128)(2,1)S(1)} %bitcast.9) | data formatting | bytes 2097152 | tf_op jit(solution)/shard_map/reshape | solution.py:190
  57.7 0.0 copy-done.7
  57.7 2.2 %collective-permute-done.5.ox_ref = bf16[128,512]{1,0:T(8,128)(2,1)S(1)} collective-permute-done((bf16[128,512]{1,0:T(8,128)(2,1)S(1)}, bf16[128,512]{1,0:T(8,128)(2,1)S(1)}, u32[]{:S(2)}, u32[]{:S(2)}) %collective-permute-start.5) | collective-permute-done | bytes 131104 | tf_op jit(solution)/shard_map/ppermute | solution.py:164
  59.8 2.2 %collective-permute-done.6.sx_ref = bf16[128,512]{1,0:T(8,128)(2,1)S(1)} collective-permute-done((bf16[128,512]{1,0:T(8,128)(2,1)S(1)}, bf16[128,512]{1,0:T(8,128)(2,1)S(1)}, u32[]{:S(2)}, u32[]{:S(2)}) %collective-permute-start.6) | collective-permute-done | bytes 131104 | tf_op jit(solution)/shard_map/ppermute | solution.py:164
  62.1 0.0 copy-done.8
  62.1 0.6 copy-done.9
  62.7 2.2 %shard_map.97 = (f32[256,256]{1,0:T(8,128)}, bf16[256,256]{1,0:T(8,128)(2,1)}, bf16[256,256]{1,0:T(8,128)(2,1)}) custom-call(s32[1]{0:T(128)S(6)} %copy.11.c_ref, s32[32]{0:T(128)} %n_ref.1, s32[32,256]{1,0:T(8,128)} %pl_ref.1, bf16[1,256,512]{2,1,0:T(8,128)(2,1)} %pd_ref.1, bf16[1,512]{1,0:T(2,128)(2,1)} %reshape.20.cou_ref, bf16[128,512]{1,0:T(8,128)(2,1)} %bitcast.12, ...), custom_call_target="tpu_custom_call" | custom-call | flops 67108864 | bytes 1048576 | tf_op jit(solution)/shard_map/pallas_call | solution.py:122
  65.0 2.6 %all-to-all-done.y_ref = bf16[8,64,512]{2,1,0:T(8,128)(2,1)S(1)} async-done(((bf16[8,64,512]{2,1,0:T(8,128)(2,1)}), bf16[8,64,512]{2,1,0:T(8,128)(2,1)S(1)}, u32[]{:S(2)}, u32[]{:S(2)}) %all-to-all-start) | async-done | bytes 524320 | tf_op jit(solution)/shard_map/all_to_all | solution.py:186
  67.5 0.8 copy-done
  68.3 3.5 %shard_map.98 = bf16[256,256]{1,0:T(8,128)(2,1)} custom-call(bf16[8,64,512]{2,1,0:T(8,128)(2,1)} %copy-done, bf16[1024,512]{1,0:T(8,128)(2,1)} %bitcast.8, f32[256,256]{1,0:T(8,128)} %get-tuple-element.8.ex_ref, bf16[256,256]{1,0:T(8,128)(2,1)} %get-tuple-element.9.pt_ref), custom_call_target="tpu_custom_call" | custom-call | flops 67108864 | bytes 2097152 | tf_op jit(solution)/shard_map/pallas_call | solution.py:145
  71.8 11.3 %all_to_all.21.in_ref = bf16[8,32,256]{2,1,0:T(8,128)(2,1)} all-to-all(bf16[8,32,256]{2,1,0:T(8,128)(2,1)} %bitcast.13), channel_id=1, replica_groups=mesh['xh'=2,'z'=8,'core'=2,'xl'=2,'y'=4] {'xl','y'}, dimensions={0} | all-to-all | bytes 262144 | tf_op jit(solution)/shard_map/all_to_all | solution.py:192
  83.1 1.7 %shard_map.99 = bf16[32,256]{1,0:T(8,128)(2,1)} custom-call(bf16[8,32,256]{2,1,0:T(8,128)(2,1)} %all_to_all.21.in_ref, bf16[256,256]{1,0:T(8,128)(2,1)} %get-tuple-element.10.ps_ref), custom_call_target="tpu_custom_call" | custom-call | flops 1048576 | bytes 1048576 | tf_op jit(solution)/shard_map/pallas_call | solution.py:160
  (6 shorter events, 0.0 us)
Async XLA Ops:
  2.7 3.2 %collective-permute-start.1 = (bf16[8,64,512]{2,1,0:T(8,128)(2,1)}, bf16[8,64,512]{2,1,0:T(8,128)(2,1)S(1)}, u32[]{:S(2)}, u32[]{:S(2)}) collective-permute-start(bf16[8,64,512]{2,1,0:T(8,128)(2,1)} %shard_map.93), channel_id=1, source_target_pairs={{0,8},{8,0},{1,9},{9,1},{2,10},{10,2},{3,11},{11,3},{4,12},{12,4},... | collective-permute-start | bytes 1572872 | tf_op jit(solution)/shard_map/ppermute | solution.py:164
  5.4 6.2 %copy-start.2 = (bf16[1,256,512]{2,1,0:T(8,128)(2,1)S(1)}, bf16[1,256,512]{2,1,0:T(8,128)(2,1)}, u32[]{:S(2)}) copy-start(bf16[1,256,512]{2,1,0:T(8,128)(2,1)} %pd_ref.1) | copy-start | bytes 786436
  5.4 33.0 %collective-permute-start = (bf16[8,64,512]{2,1,0:T(8,128)(2,1)}, bf16[8,64,512]{2,1,0:T(8,128)(2,1)S(1)}, u32[]{:S(2)}, u32[]{:S(2)}) collective-permute-start(bf16[8,64,512]{2,1,0:T(8,128)(2,1)} %shard_map.91), channel_id=1, source_target_pairs={{0,8},{8,0},{1,9},{9,1},{2,10},{10,2},{3,11},{11,3},{4,12},{12,4},... | collective-permute-start | bytes 1572872 | tf_op jit(solution)/shard_map/ppermute | solution.py:164
  5.9 0.8 copy-start.5
  9.5 32.8 %collective-permute-start.2 = (bf16[8,64,512]{2,1,0:T(8,128)(2,1)}, bf16[8,64,512]{2,1,0:T(8,128)(2,1)S(1)}, u32[]{:S(2)}, u32[]{:S(2)}) collective-permute-start(bf16[8,64,512]{2,1,0:T(8,128)(2,1)} %shard_map.94), channel_id=1, source_target_pairs={{0,128},{128,0},{1,129},{129,1},{2,130},{130,2},{3,131},{131,3},{4... | collective-permute-start | bytes 1572872 | tf_op jit(solution)/shard_map/ppermute | solution.py:164
  11.7 1.5 %collective-permute-start.3 = (bf16[1,256,512]{2,1,0:T(8,128)(2,1)S(1)}, bf16[1,256,512]{2,1,0:T(8,128)(2,1)S(1)}, u32[]{:S(2)}, u32[]{:S(2)}) collective-permute-start(bf16[1,256,512]{2,1,0:T(8,128)(2,1)S(1)} %copy-done.2), channel_id=1, source_target_pairs={{0,8},{8,0},{1,9},{9,1},{2,10},{10,2},{3,11},{11,3},{4,12},{12,4},... | collective-permute-start | bytes 786440 | tf_op jit(solution)/shard_map/ppermute | solution.py:164
  13.2 0.7 copy-start.6
  35.1 12.4 %all-to-all-start.2 = ((bf16[8,16,512]{2,1,0:T(8,128)(2,1)}), bf16[8,16,512]{2,1,0:T(8,128)(2,1)S(1)}, u32[]{:S(2)}, u32[]{:S(2)}) async-start(bf16[8,16,512]{2,1,0:T(8,128)(2,1)} %shard_map.96), calls=%async_computation.2 | async-start | bytes 262144 | tf_op jit(solution)/shard_map/all_to_all | solution.py:180
  38.5 0.8 copy-start.4
  44.5 11.6 %copy-start.1 = (bf16[1,1024,512]{2,1,0:T(8,128)(2,1)S(1)}, bf16[1,1024,512]{2,1,0:T(8,128)(2,1)}, u32[]{:S(2)}) copy-start(bf16[1,1024,512]{2,1,0:T(8,128)(2,1)} %param.10) | copy-start | bytes 3145732
  47.5 4.4 %copy-start.3 = (bf16[8,16,512]{2,1,0:T(8,128)(2,1)}, bf16[8,16,512]{2,1,0:T(8,128)(2,1)S(1)}, u32[]{:S(2)}) copy-start(bf16[8,16,512]{2,1,0:T(8,128)(2,1)S(1)} %all-to-all-done.2) | copy-start | bytes 393220
  47.5 20.1 %all-to-all-start = ((bf16[8,64,512]{2,1,0:T(8,128)(2,1)}), bf16[8,64,512]{2,1,0:T(8,128)(2,1)S(1)}, u32[]{:S(2)}, u32[]{:S(2)}) async-start(bf16[8,64,512]{2,1,0:T(8,128)(2,1)} %add_convert_fusion), calls=%async_computation | async-start | bytes 1048576 | tf_op jit(solution)/shard_map/all_to_all | solution.py:186
  51.8 3.7 %copy-start.10 = (bf16[512]{0:T(512)(128)(2,1)S(1)}, bf16[512]{0:T(512)(128)(2,1)}, u32[]{:S(2)}) copy-start(bf16[512]{0:T(512)(128)(2,1)} %param.13) | copy-start | bytes 3076
  51.8 1.6 %collective-permute-start.4 = (bf16[128,512]{1,0:T(8,128)(2,1)S(1)}, bf16[128,512]{1,0:T(8,128)(2,1)S(1)}, u32[]{:S(2)}, u32[]{:S(2)}) collective-permute-start(bf16[128,512]{1,0:T(8,128)(2,1)S(1)} %bitcast.10), channel_id=1, source_target_pairs={{0,8},{8,0},{1,9},{9,1},{2,10},{10,2},{3,11},{11,3},{4,12},{12,4},... | collective-permute-start | bytes 393224 | tf_op jit(solution)/shard_map/ppermute | solution.py:164
  51.9 8.0 %collective-permute-start.5 = (bf16[128,512]{1,0:T(8,128)(2,1)S(1)}, bf16[128,512]{1,0:T(8,128)(2,1)S(1)}, u32[]{:S(2)}, u32[]{:S(2)}) collective-permute-start(bf16[128,512]{1,0:T(8,128)(2,1)S(1)} %bitcast.11), channel_id=1, source_target_pairs={{0,128},{128,0},{1,129},{129,1},{2,130},{130,2},{3,131},{131,3},{4... | collective-permute-start | bytes 393224 | tf_op jit(solution)/shard_map/ppermute | solution.py:164
  53.4 4.3 %copy-start.7 = (bf16[128,512]{1,0:T(8,128)(2,1)}, bf16[128,512]{1,0:T(8,128)(2,1)S(1)}, u32[]{:S(2)}) copy-start(bf16[128,512]{1,0:T(8,128)(2,1)S(1)} %collective-permute-done.4.sib_ref) | copy-start | bytes 393220
  53.4 8.7 %collective-permute-start.6 = (bf16[128,512]{1,0:T(8,128)(2,1)S(1)}, bf16[128,512]{1,0:T(8,128)(2,1)S(1)}, u32[]{:S(2)}, u32[]{:S(2)}) collective-permute-start(bf16[128,512]{1,0:T(8,128)(2,1)S(1)} %collective-permute-done.4.sib_ref), channel_id=1, source_target_pairs={{0,128},{128,0},{1,129},{129,1},{2,130},{130,2},{3,131},{131,3},{4... | collective-permute-start | bytes 393224 | tf_op jit(solution)/shard_map/ppermute | solution.py:164
  59.8 2.2 %copy-start.8 = (bf16[128,512]{1,0:T(8,128)(2,1)}, bf16[128,512]{1,0:T(8,128)(2,1)S(1)}, u32[]{:S(2)}) copy-start(bf16[128,512]{1,0:T(8,128)(2,1)S(1)} %collective-permute-done.5.ox_ref) | copy-start | bytes 393220
  62.1 0.6 copy-start.9
  67.5 0.8 copy-start

commit v2 on v1

v2 whole, which is shorter than its diff:
```python
import jax
import jax.numpy as jnp
from jax import lax
from jax.experimental import pallas as pl
from jax.experimental.pallas import tpu as pltpu
from jax.sharding import Mesh
from jax.sharding import PartitionSpec as P


NV = 8
NC = 32
XH, Z, CORE, XL, Y = 2, 8, 2, 2, 4
ROW = ("xh", "z", "core")
GA = ("xl", "y")
BF = jnp.bfloat16
F32 = jnp.float32
VMEM = pl.BlockSpec(memory_space=pltpu.VMEM)
SMEM = pl.BlockSpec(memory_space=pltpu.SMEM)
ANY = pl.BlockSpec(memory_space=pl.ANY)
LAST = (((1,), (1,)), ((), ()))


def near(x):
    return pltpu.with_memory_space_constraint(x, pltpu.VMEM)


def call(body, out, scalars, arrays, after=(), scratch=(), limit=12 << 20, flops=1 << 20, nbytes=1 << 20):
    many = isinstance(out, (list, tuple))
    n_in, n_after = len(scalars) + len(arrays), len(after)

    def run(*refs):
        body(*refs[:n_in], *refs[n_in + n_after :])

    return pl.pallas_call(
        run,
        out_shape=out,
        in_specs=[SMEM] * len(scalars) + [VMEM] * len(arrays) + [ANY] * n_after,
        out_specs=tuple(SMEM if o.memory_space == pltpu.SMEM else VMEM for o in out) if many else VMEM,
        scratch_shapes=list(scratch),
        compiler_params=pltpu.CompilerParams(vmem_limit_bytes=limit),
        cost_estimate=pl.CostEstimate(flops=flops, bytes_accessed=nbytes, transcendentals=0),
    )(*scalars, *arrays, *after)


def dot(a, b):
    return lax.dot_general(a, b, LAST, preferred_element_type=F32)


def partial_terms(refs, other_x, other_core, emit):
    q_ref, val_ref, w_ref = refs
    xh, core = lax.axis_index("xh"), lax.axis_index("core")
    xh = 1 - xh if other_x else xh
    core = 1 - core if other_core else core
    for z in range(Z):
        k = (xh * Z + z) * CORE + core
        emit(z, dot(val_ref[k], w_ref[q_ref[k]]))


def to_other_core(q_index, val, screened, after=()):
    def body(q_ref, val_ref, w_ref, out_ref):
        def emit(z, r):
            out_ref[z] = r.astype(BF)

        partial_terms((q_ref, val_ref, w_ref), False, True, emit)

    return call(body, pltpu.VMEM((Z, val.shape[1], screened.shape[1]), BF), [q_index], [val, screened], after)


def first_terms(q_index, val, screened):
    def body(q_ref, val_ref, w_ref, out_ref, val_out, w_out, q_out):
        def emit(z, r):
            out_ref[z] = r.astype(BF)

        for k in range(q_ref.shape[0]):
            q_out[k] = q_ref[k]

        partial_terms((q_ref, val_ref, w_ref), True, True, emit)
        val_out[...] = val_ref[...]
        w_out[...] = w_ref[...]

    out = (
        pltpu.VMEM((Z, val.shape[1], screened.shape[1]), BF),
        pltpu.VMEM(val.shape, BF),
        pltpu.VMEM(screened.shape, BF),
        pltpu.SMEM(q_index.shape, jnp.int32),
    )
    return call(body, out, [q_index], [val, screened], limit=64_400_000)


def to_other_x(q_index, val, screened, arrived, after=()):
    def body(q_ref, val_ref, w_ref, in_ref, out_ref):
        def emit(z, r):
            out_ref[z] = (r + in_ref[z].astype(F32)).astype(BF)

        partial_terms((q_ref, val_ref, w_ref), True, False, emit)

    return call(body, pltpu.VMEM(arrived.shape, BF), [q_index], [val, screened, arrived], after)


def own_terms(q_index, val, screened, arrived):
    def body(q_ref, val_ref, w_ref, in_ref, out_ref):
        def emit(z, r):
            out_ref[z] = r + in_ref[z].astype(F32)

        partial_terms((q_ref, val_ref, w_ref), False, False, emit)

    return call(body, pltpu.VMEM(arrived.shape, F32), [q_index], [val, screened, arrived])


def prepare(column, counts, pair_list, pair_dens, coulomb):
    slots, g = pair_dens.shape[1:]

    def body(c_ref, n_ref, pl_ref, pd_ref, cou_ref, weighted_ref, pt_ref, ps_ref):
        xh, z, core = (lax.axis_index(a) for a in ROW)
        k = (xh * Z + z) * CORE + core
        ck = c_ref[0]
        weighted_ref[...] = (pd_ref[0].astype(F32) * cou_ref[...].astype(F32)).astype(BF)
        pair = lax.broadcasted_iota(jnp.int32, (slots, slots), 0)
        slot = lax.broadcasted_iota(jnp.int32, (slots, slots), 1)
        mine = (pair == pl_ref[pl.ds(k, 1), :]) & (slot < n_ref[k])
        ps_ref[...] = mine.astype(F32).astype(BF)
        theirs = (pair == pl_ref[pl.ds(ck, 1), :]) & (slot < n_ref[ck])
        pt_ref[...] = theirs.astype(F32).T.astype(BF)

    out = (pltpu.VMEM((slots, g), BF), pltpu.VMEM((slots, slots), BF), pltpu.VMEM((slots, slots), BF))
    return call(body, out, [column, counts], [pair_list, pair_dens, coulomb.reshape(1, g)])


def half_of_column(column, own, sib):
    half = own.shape[1] // CORE

    def body(c_ref, own_ref, sib_ref, out_ref):
        core = lax.axis_index("core")
        rows = pl.ds(pl.multiple_of(core * half, half), half)
        mine = c_ref[0] % CORE == core

        @pl.when(mine)
        def _():
            out_ref[...] = own_ref[0, rows, :]

        @pl.when(jnp.logical_not(mine))
        def _():
            out_ref[...] = sib_ref[0, rows, :]

    return call(body, pltpu.VMEM((half, own.shape[2]), BF), [column], [own, sib])


def pick(column, own, below, above, reach, after=()):
    def body(c_ref, own_ref, below_ref, above_ref, out_ref):
        d = (lax.axis_index("z") - (c_ref[0] // CORE) % Z + Z) % Z
        low = (d > reach) & (d <= Z // 2) if reach else d == 1
        high = (d > Z // 2) & (d < Z - reach) if reach else d == Z - 1

        @pl.when(low)
        def _():
            out_ref[...] = below_ref[...]

        @pl.when(high)
        def _():
            out_ref[...] = above_ref[...]

        @pl.when(jnp.logical_not(low | high))
        def _():
            out_ref[...] = own_ref[...]

    return call(body, pltpu.VMEM(own.shape, BF), [column], [own, below, above], after)


def pick_x(column, own, other):
    def body(c_ref, own_ref, other_ref, out_ref):
        same = c_ref[0] // (Z * CORE) == lax.axis_index("xh")

        @pl.when(same)
        def _():
            out_ref[...] = own_ref[...]

        @pl.when(jnp.logical_not(same))
        def _():
            out_ref[...] = other_ref[...]

    return call(body, pltpu.VMEM(own.shape, BF), [column], [own, other])


def add(own, arrived):
    def body(own_ref, in_ref, out_ref):
        for z in range(Z):
            out_ref[z] = (own_ref[z] + in_ref[z].astype(F32)).astype(BF)

    return call(body, pltpu.VMEM(own.shape, BF), [], [own, arrived])


def exchange_terms(weighted, own_half, sib_half):
    slots = weighted.shape[0]
    half = slots // CORE

    def body(weighted_ref, own_ref, sib_ref, ex_ref):
        own = 2.0 * dot(weighted_ref[...], own_ref[...])
        sib = 2.0 * dot(weighted_ref[...], sib_ref[...])
        low = lax.axis_index("core") == 0
        ex_ref[:, :half] = jnp.where(low, own, sib)
        ex_ref[:, half:] = jnp.where(low, sib, own)

    return call(body, pltpu.VMEM((slots, slots), F32), [], [weighted, own_half, sib_half])


def combine(arrived, cond, ex2, pt):
    slots = ex2.shape[0]
    vv = arrived.shape[1]

    def body(y_ref, cond_ref, ex_ref, pt_ref, out_ref, s_ref):
        sv = jnp.sum(y_ref[...].astype(F32), axis=0).astype(BF)
        i = lax.broadcasted_iota(jnp.int32, (vv, vv), 0)
        j = lax.broadcasted_iota(jnp.int32, (vv, vv), 1)
        turn = (j == (i % NV) * NV + i // NV).astype(F32).astype(BF)
        sv = jnp.dot(turn, sv, preferred_element_type=F32).astype(BF)
        r = dot(sv, cond_ref[0])
        for c in range(NC):
            s_ref[pl.ds(c, vv, stride=NC), :] = r[:, c * NC : (c + 1) * NC]
        direct = jnp.concatenate([s_ref[v * slots : (v + 1) * slots, :] for v in range(NV)], axis=1)
        terms = (ex_ref[...] - direct).astype(BF)
        out_ref[...] = dot(pt_ref[...], terms).astype(BF)

    return call(
        body, pltpu.VMEM((slots, slots), BF), [], [arrived, cond, ex2, pt], (), [pltpu.VMEM((vv * NC, NC), F32)]
    )


def finish(parts, ps):
    def body(in_ref, ps_ref, out_ref):
        total = jnp.sum(in_ref[...].astype(F32), axis=0).astype(BF)
        out_ref[...] = jnp.dot(total, ps_ref[...], preferred_element_type=F32).astype(BF)

    return call(body, jax.ShapeDtypeStruct(parts.shape[1:], BF), [], [parts, ps])


def shift(x, axis, size, by):
    return lax.ppermute(x, axis, [(i, (i + by) % size) for i in range(size)])


def swap(x, axis):
    return shift(x, axis, 2, 1)


def per_device(
    pair_dens, cond_dens, val_dens, screened, coulomb, pair_list, counts, q_index, column_k
):
    slots = pair_dens.shape[1]
    sib = swap(pair_dens, "core")
    to_core, val_near, screened_near, q_index = first_terms(q_index, val_dens, screened)
    from_core = swap(to_core, "core")
    to_x = to_other_x(q_index, val_near, screened_near, near(from_core))
    from_x = swap(to_x, "xh")
    to_core = to_other_core(q_index, val_near, screened_near, (to_x,))
    from_core_2 = swap(to_core, "core")
    own = own_terms(q_index, val_near, screened_near, near(from_core_2))
    weighted, pt, ps = prepare(column_k, counts, pair_list, pair_dens, coulomb)
    half = half_of_column(column_k, near(pair_dens), near(sib))
    ups, downs = (shift(half, "z", Z, by) for by in (1, -1))
    once = pick(column_k, half, near(ups), near(downs), 0)
    ups, downs = (shift(once, "z", Z, by) for by in (3, -3))
    own_half = pick(column_k, once, near(ups), near(downs), 1)
    own_half = pick_x(column_k, own_half, near(swap(own_half, "xh")))
    sib_half = swap(own_half, "core")
    to_z = add(own, near(from_x))
    arrived = lax.all_to_all(to_z, "z", 0, 0, tiled=True)
    ex2 = exchange_terms(weighted, own_half, near(sib_half))
    combined = combine(near(arrived), near(cond_dens), ex2, pt)
    blocks = lax.all_to_all(combined.reshape(XL * Y, -1, slots), GA, 0, 0, tiled=True)
    return finish(near(blocks), ps).T


def solution(mesh):
    fine = Mesh(mesh.devices.reshape(XH, Z, CORE, XL, Y), ROW + GA)
    placed = (
        P(ROW, None, GA),
        P(ROW, None, GA),
        P(None, None, ROW),
        P(None, GA, ROW),
        P(GA),
        P(),
        P(),
        P(),
        P(),
    )

    return jax.shard_map(per_device, mesh=fine, in_specs=placed, out_specs=P(ROW, GA), check_vma=False)
```

time: 85.5 us -> 85.5 us (level)
  the two profiles are of different devices: /device:TPU:2 before, /device:TPU:32 now
where the time goes in v2:
time: 85.5 us; the launch traced here: 85.2 us
  waiting for transfers between devices  42.6 us (50%)
  starting transfers between devices  22.5 us (26%)
  blocking collectives  11.8 us (14%)
  Pallas kernels  7.54 us (9%)
    ppermute x10, waiting for transfers between devices, shift(): return lax.ppermute(x, axis, [(i, (i + by) % size) for i in range(size)])  42.6 us
    ppermute x10, starting transfers between devices, shift(): return lax.ppermute(x, axis, [(i, (i + by) % size) for i in range(size)])  13.8 us
    all_to_all x1, blocking collectives, per_device(): lax.all_to_all(combined.reshape(XL * Y, -1, slots), GA, 0, 0, tiled=True)  11.8 us
    all_to_all x1, starting transfers between devices, per_device(): arrived = lax.all_to_all(to_z, 'z', 0, 0, tiled=True)  8.7 us
    pallas_call x13, Pallas kernels, call(): pl.pallas_call(run, out_shape=out, in_specs=[SMEM] * len(scalars) + [VMEM...  7.54 us
  transfers between devices with their start and end apart: 11, of which 9 were waited for; matrix products, arithmetic and copies ran while one was open for 0% of the time, Pallas kernels for 2%

profile of v2, /device:TPU:32, one launch (start us, length us, event | category | flops | bytes accessed | tf_op | source)
XLA Modules:
  0.0 85.2 jit_solution(9341770987353497335)
XLA Ops:
  0.0 1.9 %shard_map.91 = (bf16[8,64,512]{2,1,0:T(8,128)(2,1)S(1)}, bf16[32,64,128]{2,1,0:T(8,128)(2,1)S(1)}, bf16[8,512,128]{2,1,0:T(8,128)(2,1)S(1)}, s32[32]{0:T(128)S(4)}) custom-call(s32[32]{0:T(128)} %refs_0_.6, bf16[32,64,128]{2,1,0:T(8,128)(2,1)} %refs_1_.4, bf16[8,512,128]{2,1,0:T(8,128)(2,1)} %refs_2_.2), custom_call_target="tpu_custom_call" | custom-call | flops 1048576 | bytes 1048576 | tf_op jit(solution)/shard_map/pallas_call | solution.py:34
  1.9 0.1 collective-permute-start
  2.0 1.9 %collective-permute-done.refs_3_ = bf16[8,64,512]{2,1,0:T(8,128)(2,1)S(1)} collective-permute-done((bf16[8,64,512]{2,1,0:T(8,128)(2,1)S(1)}, bf16[8,64,512]{2,1,0:T(8,128)(2,1)S(1)}, u32[]{:S(2)}, u32[]{:S(2)}) %collective-permute-start) | collective-permute-done | bytes 524320 | tf_op jit(solution)/shard_map/ppermute | solution.py:237
  3.9 0.5 shard_map.92.refs_3_
  4.4 0.5 shard_map.93
  4.9 0.2 collective-permute-start.1
  5.1 3.0 %collective-permute-start.2 = (bf16[8,64,512]{2,1,0:T(8,128)(2,1)S(1)}, bf16[8,64,512]{2,1,0:T(8,128)(2,1)S(1)}, u32[]{:S(2)}, u32[]{:S(2)}) collective-permute-start(bf16[8,64,512]{2,1,0:T(8,128)(2,1)S(1)} %shard_map.92.refs_3_), channel_id=1, source_target_pairs={{0,128},{128,0},{1,129},{129,1},{2,130},{130,2},{3,131},{131,3},{4... | collective-permute-start | bytes 1572872 | tf_op jit(solution)/shard_map/ppermute | solution.py:237
  8.2 0.0 collective-permute-done.1.refs_3_
  8.2 0.5 shard_map.94.refs_0_
  8.7 12.2 %collective-permute-done.2.refs_1_ = bf16[8,64,512]{2,1,0:T(8,128)(2,1)S(1)} collective-permute-done((bf16[8,64,512]{2,1,0:T(8,128)(2,1)S(1)}, bf16[8,64,512]{2,1,0:T(8,128)(2,1)S(1)}, u32[]{:S(2)}, u32[]{:S(2)}) %collective-permute-start.2) | collective-permute-done | bytes 524320 | tf_op jit(solution)/shard_map/ppermute | solution.py:237
  20.9 0.9 %shard_map.95 = bf16[8,64,512]{2,1,0:T(8,128)(2,1)} custom-call(f32[8,64,512]{2,1,0:T(8,128)S(1)} %shard_map.94.refs_0_, bf16[8,64,512]{2,1,0:T(8,128)(2,1)S(1)} %collective-permute-done.2.refs_1_), custom_call_target="tpu_custom_call" | custom-call | flops 1048576 | bytes 1048576 | tf_op jit(solution)/shard_map/pallas_call | solution.py:34
  21.8 0.0 copy-start.1
  21.8 8.7 %all-to-all-start = ((bf16[8,64,512]{2,1,0:T(8,128)(2,1)}), bf16[8,64,512]{2,1,0:T(8,128)(2,1)S(1)}, u32[]{:S(2)}, u32[]{:S(2)}) async-start(bf16[8,64,512]{2,1,0:T(8,128)(2,1)} %shard_map.95), calls=%async_computation | async-start | bytes 1048576 | tf_op jit(solution)/shard_map/all_to_all | solution.py:265
  30.5 0.0 copy-done.1
  30.5 0.0 collective-permute-start.3
  31.1 0.9 %collective-permute-done.3.refs_2_ = bf16[1,256,512]{2,1,0:T(8,128)(2,1)S(1)} collective-permute-done((bf16[1,256,512]{2,1,0:T(8,128)(2,1)S(1)}, bf16[1,256,512]{2,1,0:T(8,128)(2,1)S(1)}, u32[]{:S(2)}, u32[]{:S(2)}) %collective-permute-start.3) | collective-permute-done | bytes 262176 | tf_op jit(solution)/shard_map/ppermute | solution.py:237
  32.0 1.5 %collective-permute-start.4 = (bf16[128,512]{1,0:T(8,128)(2,1)S(1)}, bf16[128,512]{1,0:T(8,128)(2,1)S(1)}, u32[]{:S(2)}, u32[]{:S(2)}) collective-permute-start(bf16[128,512]{1,0:T(8,128)(2,1)S(1)} %shard_map.97.refs_1_), channel_id=1, source_target_pairs={{0,16},{16,32},{32,48},{48,64},{64,80},{80,96},{96,112},{112,0},{1... | collective-permute-start | bytes 393224 | tf_op jit(solution)/shard_map/ppermute | solution.py:237
  33.6 0.6 collective-permute-start.5
  34.1 10.4 %collective-permute-done.4.refs_2_ = bf16[128,512]{1,0:T(8,128)(2,1)S(1)} collective-permute-done((bf16[128,512]{1,0:T(8,128)(2,1)S(1)}, bf16[128,512]{1,0:T(8,128)(2,1)S(1)}, u32[]{:S(2)}, u32[]{:S(2)}) %collective-permute-start.4) | collective-permute-done | bytes 131104 | tf_op jit(solution)/shard_map/ppermute | solution.py:237
  44.5 0.5 collective-permute-done.5.refs_3_
  45.0 0.0 copy-start.4
  45.0 0.0 copy-start.2
  45.0 0.0 copy-start.3
  45.0 0.0 copy-start
  45.0 4.7 %collective-permute-start.6 = (bf16[128,512]{1,0:T(8,128)(2,1)S(1)}, bf16[128,512]{1,0:T(8,128)(2,1)S(1)}, u32[]{:S(2)}, u32[]{:S(2)}) collective-permute-start(bf16[128,512]{1,0:T(8,128)(2,1)S(1)} %shard_map.98.refs_1_), channel_id=1, source_target_pairs={{0,48},{16,64},{32,80},{48,96},{64,112},{80,0},{96,16},{112,32},{1... | collective-permute-start | bytes 393224 | tf_op jit(solution)/shard_map/ppermute | solution.py:237
  49.7 0.5 collective-permute-start.7
  50.2 7.5 %collective-permute-done.6.refs_2_ = bf16[128,512]{1,0:T(8,128)(2,1)S(1)} collective-permute-done((bf16[128,512]{1,0:T(8,128)(2,1)S(1)}, bf16[128,512]{1,0:T(8,128)(2,1)S(1)}, u32[]{:S(2)}, u32[]{:S(2)}) %collective-permute-start.6) | collective-permute-done | bytes 131104 | tf_op jit(solution)/shard_map/ppermute | solution.py:237
  57.6 5.2 %collective-permute-done.7.refs_3_ = bf16[128,512]{1,0:T(8,128)(2,1)S(1)} collective-permute-done((bf16[128,512]{1,0:T(8,128)(2,1)S(1)}, bf16[128,512]{1,0:T(8,128)(2,1)S(1)}, u32[]{:S(2)}, u32[]{:S(2)}) %collective-permute-start.7) | collective-permute-done | bytes 131104 | tf_op jit(solution)/shard_map/ppermute | solution.py:237
  62.9 3.1 %collective-permute-start.8 = (bf16[128,512]{1,0:T(8,128)(2,1)S(1)}, bf16[128,512]{1,0:T(8,128)(2,1)S(1)}, u32[]{:S(2)}, u32[]{:S(2)}) collective-permute-start(bf16[128,512]{1,0:T(8,128)(2,1)S(1)} %shard_map.99.refs_1_), channel_id=1, source_target_pairs={{0,128},{128,0},{1,129},{129,1},{2,130},{130,2},{3,131},{131,3},{4... | collective-permute-start | bytes 393224 | tf_op jit(solution)/shard_map/ppermute | solution.py:237
  66.0 3.4 %collective-permute-done.8.refs_2_ = bf16[128,512]{1,0:T(8,128)(2,1)S(1)} collective-permute-done((bf16[128,512]{1,0:T(8,128)(2,1)S(1)}, bf16[128,512]{1,0:T(8,128)(2,1)S(1)}, u32[]{:S(2)}, u32[]{:S(2)}) %collective-permute-start.8) | collective-permute-done | bytes 131104 | tf_op jit(solution)/shard_map/ppermute | solution.py:237
  69.5 0.1 collective-permute-start.9
  69.6 0.0 copy-done.4
  69.6 0.0 copy-done.2
  69.6 0.0 copy-done.3
  69.6 0.7 shard_map.96
  70.3 0.6 collective-permute-done.9.refs_2_
  70.9 0.3 shard_map.101.refs_2_
  71.2 0.0 all-to-all-done.refs_0_
  71.2 0.0 copy-done
  71.2 1.5 %shard_map.102 = bf16[256,256]{1,0:T(8,128)(2,1)S(1)} custom-call(bf16[8,64,512]{2,1,0:T(8,128)(2,1)S(1)} %all-to-all-done.refs_0_, bf16[1,1024,512]{2,1,0:T(8,128)(2,1)S(1)} %copy-done, f32[256,256]{1,0:T(8,128)S(1)} %shard_map.101.refs_2_, bf16[256,256]{1,0:T(8,128)(2,1)S(1)} %get-tuple-element.17.refs_3_), custom_call_target="tpu_custom_call" | custom-call | flops 1048576 | bytes 1048576 | tf_op jit(solution)/shard_map/pallas_call | solution.py:34
  72.7 11.8 %all_to_all.10.refs_0_ = bf16[8,32,256]{2,1,0:T(8,128)(2,1)S(1)} all-to-all(bf16[8,32,256]{2,1,0:T(8,128)(2,1)S(1)} %bitcast.2), channel_id=1, replica_groups=mesh['xh'=2,'z'=8,'core'=2,'xl'=2,'y'=4] {'xl','y'}, dimensions={0} | all-to-all | bytes 262144 | tf_op jit(solution)/shard_map/all_to_all | solution.py:268
  84.5 0.8 shard_map.103
  (5 shorter events, 0.1 us)
Async XLA Ops:
  1.9 2.0 %collective-permute-start = (bf16[8,64,512]{2,1,0:T(8,128)(2,1)S(1)}, bf16[8,64,512]{2,1,0:T(8,128)(2,1)S(1)}, u32[]{:S(2)}, u32[]{:S(2)}) collective-permute-start(bf16[8,64,512]{2,1,0:T(8,128)(2,1)S(1)} %get-tuple-element.15), channel_id=1, source_target_pairs={{0,8},{8,0},{1,9},{9,1},{2,10},{10,2},{3,11},{11,3},{4,12},{12,4},... | collective-permute-start | bytes 1572872 | tf_op jit(solution)/shard_map/ppermute | solution.py:237
  4.9 3.2 %collective-permute-start.1 = (bf16[8,64,512]{2,1,0:T(8,128)(2,1)S(1)}, bf16[8,64,512]{2,1,0:T(8,128)(2,1)S(1)}, u32[]{:S(2)}, u32[]{:S(2)}) collective-permute-start(bf16[8,64,512]{2,1,0:T(8,128)(2,1)S(1)} %shard_map.93), channel_id=1, source_target_pairs={{0,8},{8,0},{1,9},{9,1},{2,10},{10,2},{3,11},{11,3},{4,12},{12,4},... | collective-permute-start | bytes 1572872 | tf_op jit(solution)/shard_map/ppermute | solution.py:237
  5.1 15.7 %collective-permute-start.2 = (bf16[8,64,512]{2,1,0:T(8,128)(2,1)S(1)}, bf16[8,64,512]{2,1,0:T(8,128)(2,1)S(1)}, u32[]{:S(2)}, u32[]{:S(2)}) collective-permute-start(bf16[8,64,512]{2,1,0:T(8,128)(2,1)S(1)} %shard_map.92.refs_3_), channel_id=1, source_target_pairs={{0,128},{128,0},{1,129},{129,1},{2,130},{130,2},{3,131},{131,3},{4... | collective-permute-start | bytes 1572872 | tf_op jit(solution)/shard_map/ppermute | solution.py:237
  21.8 8.7 %copy-start.1 = (bf16[1,256,512]{2,1,0:T(8,128)(2,1)S(1)}, bf16[1,256,512]{2,1,0:T(8,128)(2,1)}, u32[]{:S(2)}) copy-start(bf16[1,256,512]{2,1,0:T(8,128)(2,1)} %refs_1_.6) | copy-start | bytes 786436
  21.8 49.4 %all-to-all-start = ((bf16[8,64,512]{2,1,0:T(8,128)(2,1)}), bf16[8,64,512]{2,1,0:T(8,128)(2,1)S(1)}, u32[]{:S(2)}, u32[]{:S(2)}) async-start(bf16[8,64,512]{2,1,0:T(8,128)(2,1)} %shard_map.95), calls=%async_computation | async-start | bytes 1048576 | tf_op jit(solution)/shard_map/all_to_all | solution.py:265
  30.5 1.5 %collective-permute-start.3 = (bf16[1,256,512]{2,1,0:T(8,128)(2,1)S(1)}, bf16[1,256,512]{2,1,0:T(8,128)(2,1)S(1)}, u32[]{:S(2)}, u32[]{:S(2)}) collective-permute-start(bf16[1,256,512]{2,1,0:T(8,128)(2,1)S(1)} %copy-done.1), channel_id=1, source_target_pairs={{0,8},{8,0},{1,9},{9,1},{2,10},{10,2},{3,11},{11,3},{4,12},{12,4},... | collective-permute-start | bytes 786440 | tf_op jit(solution)/shard_map/ppermute | solution.py:237
  32.0 12.5 %collective-permute-start.4 = (bf16[128,512]{1,0:T(8,128)(2,1)S(1)}, bf16[128,512]{1,0:T(8,128)(2,1)S(1)}, u32[]{:S(2)}, u32[]{:S(2)}) collective-permute-start(bf16[128,512]{1,0:T(8,128)(2,1)S(1)} %shard_map.97.refs_1_), channel_id=1, source_target_pairs={{0,16},{16,32},{32,48},{48,64},{64,80},{80,96},{96,112},{112,0},{1... | collective-permute-start | bytes 393224 | tf_op jit(solution)/shard_map/ppermute | solution.py:237
  33.6 11.5 %collective-permute-start.5 = (bf16[128,512]{1,0:T(8,128)(2,1)S(1)}, bf16[128,512]{1,0:T(8,128)(2,1)S(1)}, u32[]{:S(2)}, u32[]{:S(2)}) collective-permute-start(bf16[128,512]{1,0:T(8,128)(2,1)S(1)} %shard_map.97.refs_1_), channel_id=1, source_target_pairs={{0,112},{16,0},{32,16},{48,32},{64,48},{80,64},{96,80},{112,96},{1... | collective-permute-start | bytes 393224 | tf_op jit(solution)/shard_map/ppermute | solution.py:237
  45.0 24.6 %copy-start.4 = (bf16[512]{0:T(512)(128)(2,1)S(1)}, bf16[512]{0:T(512)(128)(2,1)}, u32[]{:S(2)}) copy-start(bf16[512]{0:T(512)(128)(2,1)} %param.13) | copy-start | bytes 3076
  45.0 24.6 %copy-start.2 = (s32[32,256]{1,0:T(8,128)S(1)}, s32[32,256]{1,0:T(8,128)}, u32[]{:S(2)}) copy-start(s32[32,256]{1,0:T(8,128)} %refs_2_.3) | copy-start | bytes 98308
  45.0 24.6 %copy-start.3 = (s32[32]{0:T(128)S(1)}, s32[32]{0:T(128)}, u32[]{:S(2)}) copy-start(s32[32]{0:T(128)} %refs_1_.5) | copy-start | bytes 388
  45.0 26.2 %copy-start = (bf16[1,1024,512]{2,1,0:T(8,128)(2,1)S(1)}, bf16[1,1024,512]{2,1,0:T(8,128)(2,1)}, u32[]{:S(2)}) copy-start(bf16[1,1024,512]{2,1,0:T(8,128)(2,1)} %refs_1_.7) | copy-start | bytes 3145732
  45.0 12.6 %collective-permute-start.6 = (bf16[128,512]{1,0:T(8,128)(2,1)S(1)}, bf16[128,512]{1,0:T(8,128)(2,1)S(1)}, u32[]{:S(2)}, u32[]{:S(2)}) collective-permute-start(bf16[128,512]{1,0:T(8,128)(2,1)S(1)} %shard_map.98.refs_1_), channel_id=1, source_target_pairs={{0,48},{16,64},{32,80},{48,96},{64,112},{80,0},{96,16},{112,32},{1... | collective-permute-start | bytes 393224 | tf_op jit(solution)/shard_map/ppermute | solution.py:237
  49.7 13.2 %collective-permute-start.7 = (bf16[128,512]{1,0:T(8,128)(2,1)S(1)}, bf16[128,512]{1,0:T(8,128)(2,1)S(1)}, u32[]{:S(2)}, u32[]{:S(2)}) collective-permute-start(bf16[128,512]{1,0:T(8,128)(2,1)S(1)} %shard_map.98.refs_1_), channel_id=1, source_target_pairs={{0,80},{16,96},{32,112},{48,0},{64,16},{80,32},{96,48},{112,64},{1... | collective-permute-start | bytes 393224 | tf_op jit(solution)/shard_map/ppermute | solution.py:237
  62.9 6.6 %collective-permute-start.8 = (bf16[128,512]{1,0:T(8,128)(2,1)S(1)}, bf16[128,512]{1,0:T(8,128)(2,1)S(1)}, u32[]{:S(2)}, u32[]{:S(2)}) collective-permute-start(bf16[128,512]{1,0:T(8,128)(2,1)S(1)} %shard_map.99.refs_1_), channel_id=1, source_target_pairs={{0,128},{128,0},{1,129},{129,1},{2,130},{130,2},{3,131},{131,3},{4... | collective-permute-start | bytes 393224 | tf_op jit(solution)/shard_map/ppermute | solution.py:237
  69.5 1.4 %collective-permute-start.9 = (bf16[128,512]{1,0:T(8,128)(2,1)S(1)}, bf16[128,512]{1,0:T(8,128)(2,1)S(1)}, u32[]{:S(2)}, u32[]{:S(2)}) collective-permute-start(bf16[128,512]{1,0:T(8,128)(2,1)S(1)} %shard_map.100.refs_1_), channel_id=1, source_target_pairs={{0,8},{8,0},{1,9},{9,1},{2,10},{10,2},{3,11},{11,3},{4,12},{12,4},... | collective-permute-start | bytes 393224 | tf_op jit(solution)/shard_map/ppermute | solution.py:237

commit v3 on v2

--- a/solution.py
+++ b/solution.py
@@ -46,12 +46,12 @@
     return lax.dot_general(a, b, LAST, preferred_element_type=F32)
 
 
-def partial_terms(refs, other_x, other_core, emit):
+def partial_terms(refs, other_x, other_core, emit, planes=range(Z)):
     q_ref, val_ref, w_ref = refs
     xh, core = lax.axis_index("xh"), lax.axis_index("core")
     xh = 1 - xh if other_x else xh
     core = 1 - core if other_core else core
-    for z in range(Z):
+    for z in planes:
         k = (xh * Z + z) * CORE + core
         emit(z, dot(val_ref[k], w_ref[q_ref[k]]))
 
@@ -67,9 +67,11 @@
 
 
 def first_terms(q_index, val, screened):
-    def body(q_ref, val_ref, w_ref, out_ref, val_out, w_out, q_out):
-        def emit(z, r):
-            out_ref[z] = r.astype(BF)
+    half = Z // 2
+
+    def body(q_ref, val_ref, w_ref, low_ref, high_ref, val_out, w_out, q_out):
+        def emit(z, r):
+            (low_ref if z < half else high_ref)[z % half] = r.astype(BF)
 
         for k in range(q_ref.shape[0]):
             q_out[k] = q_ref[k]
@@ -79,7 +81,8 @@
         w_out[...] = w_ref[...]
 
     out = (
-        pltpu.VMEM((Z, val.shape[1], screened.shape[1]), BF),
+        pltpu.VMEM((half, val.shape[1], screened.shape[1]), BF),
+        pltpu.VMEM((half, val.shape[1], screened.shape[1]), BF),
         pltpu.VMEM(val.shape, BF),
         pltpu.VMEM(screened.shape, BF),
         pltpu.SMEM(q_index.shape, jnp.int32),
@@ -87,12 +90,14 @@
     return call(body, out, [q_index], [val, screened], limit=64_400_000)
 
 
-def to_other_x(q_index, val, screened, arrived, after=()):
+def to_other_x(q_index, val, screened, arrived, part, after=()):
+    half = arrived.shape[0]
+
     def body(q_ref, val_ref, w_ref, in_ref, out_ref):
         def emit(z, r):
-            out_ref[z] = (r + in_ref[z].astype(F32)).astype(BF)
-
-        partial_terms((q_ref, val_ref, w_ref), True, False, emit)
+            out_ref[z % half] = (r + in_ref[z % half].astype(F32)).astype(BF)
+
+        partial_terms((q_ref, val_ref, w_ref), True, False, emit, range(part * half, (part + 1) * half))
 
     return call(body, pltpu.VMEM(arrived.shape, BF), [q_index], [val, screened, arrived], after)
 
@@ -166,41 +171,42 @@
     return call(body, pltpu.VMEM(own.shape, BF), [column], [own, below, above], after)
 
 
-def pick_x(column, own, other):
-    def body(c_ref, own_ref, other_ref, out_ref):
+def add(own, low, high):
+    half = low.shape[0]
+
+    def body(own_ref, low_ref, high_ref, out_ref):
+        for z in range(Z):
+            arrived = (low_ref if z < half else high_ref)[z % half]
+            out_ref[z] = (own_ref[z] + arrived.astype(F32)).astype(BF)
+
+    return call(body, pltpu.VMEM(own.shape, BF), [], [own, low, high])
+
+
+def exchange_terms(column, weighted, halves):
+    slots, g = weighted.shape
+    half = slots // CORE
+
+    def body(c_ref, weighted_ref, own_ref, sib_ref, own_x_ref, sib_x_ref, ex_ref, col_ref):
+        core = lax.axis_index("core")
         same = c_ref[0] // (Z * CORE) == lax.axis_index("xh")
+        first = pl.ds(pl.multiple_of(core * half, half), half)
+        second = pl.ds(pl.multiple_of((1 - core) * half, half), half)
 
         @pl.when(same)
         def _():
-            out_ref[...] = own_ref[...]
+            col_ref[first, :] = own_ref[...]
+            col_ref[second, :] = sib_ref[...]
 
         @pl.when(jnp.logical_not(same))
         def _():
-            out_ref[...] = other_ref[...]
-
-    return call(body, pltpu.VMEM(own.shape, BF), [column], [own, other])
-
-
-def add(own, arrived):
-    def body(own_ref, in_ref, out_ref):
-        for z in range(Z):
-            out_ref[z] = (own_ref[z] + in_ref[z].astype(F32)).astype(BF)
-
-    return call(body, pltpu.VMEM(own.shape, BF), [], [own, arrived])
-
-
-def exchange_terms(weighted, own_half, sib_half):
-    slots = weighted.shape[0]
-    half = slots // CORE
-
-    def body(weighted_ref, own_ref, sib_ref, ex_ref):
-        own = 2.0 * dot(weighted_ref[...], own_ref[...])
-        sib = 2.0 * dot(weighted_ref[...], sib_ref[...])
-        low = lax.axis_index("core") == 0
-        ex_ref[:, :half] = jnp.where(low, own, sib)
-        ex_ref[:, half:] = jnp.where(low, sib, own)
-
-    return call(body, pltpu.VMEM((slots, slots), F32), [], [weighted, own_half, sib_half])
+            col_ref[first, :] = own_x_ref[...]
+            col_ref[second, :] = sib_x_ref[...]
+
+        ex_ref[...] = 2.0 * dot(weighted_ref[...], col_ref[...])
+
+    return call(
+        body, pltpu.VMEM((slots, slots), F32), [column], [weighted, *halves], (), [pltpu.VMEM((slots, g), BF)]
+    )
 
 
 def combine(arrived, cond, ex2, pt):
@@ -208,14 +214,14 @@
     vv = arrived.shape[1]
 
     def body(y_ref, cond_ref, ex_ref, pt_ref, out_ref, s_ref):
-        sv = jnp.sum(y_ref[...].astype(F32), axis=0).astype(BF)
-        i = lax.broadcasted_iota(jnp.int32, (vv, vv), 0)
-        j = lax.broadcasted_iota(jnp.int32, (vv, vv), 1)
-        turn = (j == (i % NV) * NV + i // NV).astype(F32).astype(BF)
-        sv = jnp.dot(turn, sv, preferred_element_type=F32).astype(BF)
-        r = dot(sv, cond_ref[0])
+        sv = y_ref[0].astype(F32)
+        for z in range(1, Z):
+            sv = sv + y_ref[z].astype(F32)
+        r = dot(sv.astype(BF), cond_ref[0])
         for c in range(NC):
-            s_ref[pl.ds(c, vv, stride=NC), :] = r[:, c * NC : (c + 1) * NC]
+            for v in range(NV):
+                block = r[v * NV : (v + 1) * NV, c * NC : (c + 1) * NC]
+                s_ref[pl.ds(v * NC + c, NV, stride=slots), :] = block
         direct = jnp.concatenate([s_ref[v * slots : (v + 1) * slots, :] for v in range(NV)], axis=1)
         terms = (ex_ref[...] - direct).astype(BF)
         out_ref[...] = dot(pt_ref[...], terms).astype(BF)
@@ -246,11 +252,14 @@
 ):
     slots = pair_dens.shape[1]
     sib = swap(pair_dens, "core")
-    to_core, val_near, screened_near, q_index = first_terms(q_index, val_dens, screened)
-    from_core = swap(to_core, "core")
-    to_x = to_other_x(q_index, val_near, screened_near, near(from_core))
-    from_x = swap(to_x, "xh")
-    to_core = to_other_core(q_index, val_near, screened_near, (to_x,))
+    low, high, val_near, screened_near, q_index = first_terms(q_index, val_dens, screened)
+    low = swap(low, "core")
+    high = swap(high, "core")
+    low = low_terms = to_other_x(q_index, val_near, screened_near, near(low), 0)
+    high = to_other_x(q_index, val_near, screened_near, near(high), 1, (low,))
+    low = swap(low, "xh")
+    high = swap(high, "xh")
+    to_core = to_other_core(q_index, val_near, screened_near, (low_terms,))
     from_core_2 = swap(to_core, "core")
     own = own_terms(q_index, val_near, screened_near, near(from_core_2))
     weighted, pt, ps = prepare(column_k, counts, pair_list, pair_dens, coulomb)
@@ -259,11 +268,13 @@
     once = pick(column_k, half, near(ups), near(downs), 0)
     ups, downs = (shift(once, "z", Z, by) for by in (3, -3))
     own_half = pick(column_k, once, near(ups), near(downs), 1)
-    own_half = pick_x(column_k, own_half, near(swap(own_half, "xh")))
+    own_x = swap(own_half, "xh")
+    sib_x = lax.ppermute(own_half, ("xh", "core"), [(i, 3 - i) for i in range(4)])
     sib_half = swap(own_half, "core")
-    to_z = add(own, near(from_x))
+    to_z = add(own, near(low), near(high))
     arrived = lax.all_to_all(to_z, "z", 0, 0, tiled=True)
-    ex2 = exchange_terms(weighted, own_half, near(sib_half))
+    halves = [near(a) for a in (own_half, sib_half, own_x, sib_x)]
+    ex2 = exchange_terms(column_k, weighted, halves)
     combined = combine(near(arrived), near(cond_dens), ex2, pt)
     blocks = lax.all_to_all(combined.reshape(XL * Y, -1, slots), GA, 0, 0, tiled=True)
     return finish(near(blocks), ps).T

time: 85.5 us -> 86.4 us (1.011)
  starting transfers between devices: 22.5 us -> 24.9 us
  waiting for transfers between devices: 42.6 us -> 41.6 us
    ppermute x10 -> x12, waiting for transfers between devices: 42.6 us -> 38.9 us  [shift(): return lax.ppermute(x, axis, [(i, (i + by) % size) for i in range(size)])]
    ppermute x0 -> x1, waiting for transfers between devices: none -> 2.69 us  [per_device(): lax.ppermute(own_half, ('xh', 'core'), [(i, 3 - i) for i in range(4)])]
    ppermute x10 -> x12, starting transfers between devices: 13.8 us -> 16 us  [shift(): return lax.ppermute(x, axis, [(i, (i + by) % size) for i in range(size)])]
  transfers between devices with their start and end apart: 11 -> 14, of which waited for: 9 -> 10; matrix products, arithmetic and copies ran while one was open for 0% -> 0% of each run, Pallas kernels for 2% -> 2%
where the time goes in v3:
time: 86.4 us; the launch traced here: 86.2 us
  waiting for transfers between devices  41.6 us (48%)
  starting transfers between devices  24.9 us (29%)
  blocking collectives  11.3 us (13%)
  Pallas kernels  7.47 us (9%)
    ppermute x12, waiting for transfers between devices, shift(): return lax.ppermute(x, axis, [(i, (i + by) % size) for i in range(size)])  38.9 us
    ppermute x12, starting transfers between devices, shift(): return lax.ppermute(x, axis, [(i, (i + by) % size) for i in range(size)])  16 us
    all_to_all x1, blocking collectives, per_device(): lax.all_to_all(combined.reshape(XL * Y, -1, slots), GA, 0, 0, tiled=True)  11.3 us
    all_to_all x1, starting transfers between devices, per_device(): arrived = lax.all_to_all(to_z, 'z', 0, 0, tiled=True)  8.7 us
    pallas_call x13, Pallas kernels, call(): pl.pallas_call(run, out_shape=out, in_specs=[SMEM] * len(scalars) + [VMEM...  7.47 us
    ppermute x1, waiting for transfers between devices, per_device(): lax.ppermute(own_half, ('xh', 'core'), [(i, 3 - i) for i in range(4)])  2.69 us
  transfers between devices with their start and end apart: 14, of which 10 were waited for; matrix products, arithmetic and copies ran while one was open for 0% of the time, Pallas kernels for 2%

profile of v3, /device:TPU:32, one launch (start us, length us, event | category | flops | bytes accessed | tf_op | source)
XLA Modules:
  0.0 86.2 jit_solution(26923813160709954)
XLA Ops:
  0.0 1.9 %shard_map.91 = (bf16[4,64,512]{2,1,0:T(8,128)(2,1)S(1)}, bf16[4,64,512]{2,1,0:T(8,128)(2,1)S(1)}, bf16[32,64,128]{2,1,0:T(8,128)(2,1)S(1)}, bf16[8,512,128]{2,1,0:T(8,128)(2,1)S(1)}, s32[32]{0:T(128)S(4)}) custom-call(s32[32]{0:T(128)} %refs_0_.6, bf16[32,64,128]{2,1,0:T(8,128)(2,1)} %refs_1_.4, bf16[8,512,128]{2,1,0:T(8,128)(2,1)} %refs_2_.2), custom_call_target="tpu_custom_call" | custom-call | flops 1048576 | bytes 1048576 | tf_op jit(solution)/shard_map/pallas_call | solution.py:34
  1.9 0.1 collective-permute-start
  2.0 1.5 %collective-permute-done.refs_3_ = bf16[4,64,512]{2,1,0:T(8,128)(2,1)S(1)} collective-permute-done((bf16[4,64,512]{2,1,0:T(8,128)(2,1)S(1)}, bf16[4,64,512]{2,1,0:T(8,128)(2,1)S(1)}, u32[]{:S(2)}, u32[]{:S(2)}) %collective-permute-start) | collective-permute-done | bytes 262176 | tf_op jit(solution)/shard_map/ppermute | solution.py:243
  3.6 0.3 shard_map.92.refs_3_.refs_4_
  3.9 0.5 shard_map.93
  4.4 0.2 collective-permute-start.1
  4.6 0.4 collective-permute-start.3
  5.0 3.0 %collective-permute-start.2 = (bf16[4,64,512]{2,1,0:T(8,128)(2,1)S(1)}, bf16[4,64,512]{2,1,0:T(8,128)(2,1)S(1)}, u32[]{:S(2)}, u32[]{:S(2)}) collective-permute-start(bf16[4,64,512]{2,1,0:T(8,128)(2,1)S(1)} %shard_map.92.refs_3_.refs_4_), channel_id=1, source_target_pairs={{0,128},{128,0},{1,129},{129,1},{2,130},{130,2},{3,131},{131,3},{4... | collective-permute-start | bytes 786440 | tf_op jit(solution)/shard_map/ppermute | solution.py:243
  8.0 0.0 collective-permute-done.3.refs_3_
  8.0 0.3 shard_map.95
  8.3 1.9 %collective-permute-start.4 = (bf16[4,64,512]{2,1,0:T(8,128)(2,1)S(1)}, bf16[4,64,512]{2,1,0:T(8,128)(2,1)S(1)}, u32[]{:S(2)}, u32[]{:S(2)}) collective-permute-start(bf16[4,64,512]{2,1,0:T(8,128)(2,1)S(1)} %shard_map.95), channel_id=1, source_target_pairs={{0,128},{128,0},{1,129},{129,1},{2,130},{130,2},{3,131},{131,3},{4... | collective-permute-start | bytes 786440 | tf_op jit(solution)/shard_map/ppermute | solution.py:243
  10.2 0.0 collective-permute-done.1.refs_3_
  10.2 0.5 shard_map.94.refs_0_
  10.6 5.0 %collective-permute-done.2.refs_1_ = bf16[4,64,512]{2,1,0:T(8,128)(2,1)S(1)} collective-permute-done((bf16[4,64,512]{2,1,0:T(8,128)(2,1)S(1)}, bf16[4,64,512]{2,1,0:T(8,128)(2,1)S(1)}, u32[]{:S(2)}, u32[]{:S(2)}) %collective-permute-start.2) | collective-permute-done | bytes 262176 | tf_op jit(solution)/shard_map/ppermute | solution.py:243
  15.6 4.8 %collective-permute-done.4.refs_2_ = bf16[4,64,512]{2,1,0:T(8,128)(2,1)S(1)} collective-permute-done((bf16[4,64,512]{2,1,0:T(8,128)(2,1)S(1)}, bf16[4,64,512]{2,1,0:T(8,128)(2,1)S(1)}, u32[]{:S(2)}, u32[]{:S(2)}) %collective-permute-start.4) | collective-permute-done | bytes 262176 | tf_op jit(solution)/shard_map/ppermute | solution.py:243
  20.4 0.9 %shard_map.96 = bf16[8,64,512]{2,1,0:T(8,128)(2,1)} custom-call(f32[8,64,512]{2,1,0:T(8,128)S(1)} %shard_map.94.refs_0_, bf16[4,64,512]{2,1,0:T(8,128)(2,1)S(1)} %collective-permute-done.2.refs_1_, bf16[4,64,512]{2,1,0:T(8,128)(2,1)S(1)} %collective-permute-done.4.refs_2_), custom_call_target="tpu_custom_call" | custom-call | flops 1048576 | bytes 1048576 | tf_op jit(solution)/shard_map/pallas_call | solution.py:34
  21.3 0.0 copy-start.1
  21.3 8.7 %all-to-all-start = ((bf16[8,64,512]{2,1,0:T(8,128)(2,1)}), bf16[8,64,512]{2,1,0:T(8,128)(2,1)S(1)}, u32[]{:S(2)}, u32[]{:S(2)}) async-start(bf16[8,64,512]{2,1,0:T(8,128)(2,1)} %shard_map.96), calls=%async_computation | async-start | bytes 1048576 | tf_op jit(solution)/shard_map/all_to_all | solution.py:275
  30.0 0.0 copy-done.1
  30.0 0.0 collective-permute-start.5
  30.7 0.9 %collective-permute-done.5.refs_2_ = bf16[1,256,512]{2,1,0:T(8,128)(2,1)S(1)} collective-permute-done((bf16[1,256,512]{2,1,0:T(8,128)(2,1)S(1)}, bf16[1,256,512]{2,1,0:T(8,128)(2,1)S(1)}, u32[]{:S(2)}, u32[]{:S(2)}) %collective-permute-start.5) | collective-permute-done | bytes 262176 | tf_op jit(solution)/shard_map/ppermute | solution.py:243
  31.6 1.5 %collective-permute-start.6 = (bf16[128,512]{1,0:T(8,128)(2,1)S(1)}, bf16[128,512]{1,0:T(8,128)(2,1)S(1)}, u32[]{:S(2)}, u32[]{:S(2)}) collective-permute-start(bf16[128,512]{1,0:T(8,128)(2,1)S(1)} %shard_map.98.refs_1_), channel_id=1, source_target_pairs={{0,16},{16,32},{32,48},{48,64},{64,80},{80,96},{96,112},{112,0},{1... | collective-permute-start | bytes 393224 | tf_op jit(solution)/shard_map/ppermute | solution.py:243
  33.1 0.6 collective-permute-start.7
  33.7 10.1 %collective-permute-done.6.refs_2_ = bf16[128,512]{1,0:T(8,128)(2,1)S(1)} collective-permute-done((bf16[128,512]{1,0:T(8,128)(2,1)S(1)}, bf16[128,512]{1,0:T(8,128)(2,1)S(1)}, u32[]{:S(2)}, u32[]{:S(2)}) %collective-permute-start.6) | collective-permute-done | bytes 131104 | tf_op jit(solution)/shard_map/ppermute | solution.py:243
  43.8 0.5 collective-permute-done.7.refs_3_
  44.3 0.0 copy-start.4
  44.3 0.0 copy-start.2
  44.3 0.0 copy-start
  44.3 4.7 %collective-permute-start.8 = (bf16[128,512]{1,0:T(8,128)(2,1)S(1)}, bf16[128,512]{1,0:T(8,128)(2,1)S(1)}, u32[]{:S(2)}, u32[]{:S(2)}) collective-permute-start(bf16[128,512]{1,0:T(8,128)(2,1)S(1)} %shard_map.99.refs_1_), channel_id=1, source_target_pairs={{0,48},{16,64},{32,80},{48,96},{64,112},{80,0},{96,16},{112,32},{1... | collective-permute-start | bytes 393224 | tf_op jit(solution)/shard_map/ppermute | solution.py:243
  49.0 0.4 collective-permute-start.9
  49.5 7.5 %collective-permute-done.8.refs_2_ = bf16[128,512]{1,0:T(8,128)(2,1)S(1)} collective-permute-done((bf16[128,512]{1,0:T(8,128)(2,1)S(1)}, bf16[128,512]{1,0:T(8,128)(2,1)S(1)}, u32[]{:S(2)}, u32[]{:S(2)}) %collective-permute-start.8) | collective-permute-done | bytes 131104 | tf_op jit(solution)/shard_map/ppermute | solution.py:243
  56.9 5.3 %collective-permute-done.9.refs_3_ = bf16[128,512]{1,0:T(8,128)(2,1)S(1)} collective-permute-done((bf16[128,512]{1,0:T(8,128)(2,1)S(1)}, bf16[128,512]{1,0:T(8,128)(2,1)S(1)}, u32[]{:S(2)}, u32[]{:S(2)}) %collective-permute-start.9) | collective-permute-done | bytes 131104 | tf_op jit(solution)/shard_map/ppermute | solution.py:243
  62.2 0.1 collective-permute-start.10
  62.3 3.1 %collective-permute-start.11 = (bf16[128,512]{1,0:T(8,128)(2,1)S(1)}, bf16[128,512]{1,0:T(8,128)(2,1)S(1)}, u32[]{:S(2)}, u32[]{:S(2)}) collective-permute-start(bf16[128,512]{1,0:T(8,128)(2,1)S(1)} %shard_map.100.refs_2_), channel_id=1, source_target_pairs={{0,128},{128,0},{1,129},{129,1},{2,130},{130,2},{3,131},{131,3},{4... | collective-permute-start | bytes 393224 | tf_op jit(solution)/shard_map/ppermute | solution.py:243
  65.4 0.2 collective-permute-start.12
  65.7 0.0 copy-done.4
  65.7 0.0 copy-done.2
  65.7 0.0 copy-done.3
  65.7 0.7 shard_map.97
  66.4 0.0 collective-permute-done.10.refs_3_
  66.4 3.3 %collective-permute-done.11.refs_4_ = bf16[128,512]{1,0:T(8,128)(2,1)S(1)} collective-permute-done((bf16[128,512]{1,0:T(8,128)(2,1)S(1)}, bf16[128,512]{1,0:T(8,128)(2,1)S(1)}, u32[]{:S(2)}, u32[]{:S(2)}) %collective-permute-start.11) | collective-permute-done | bytes 131104 | tf_op jit(solution)/shard_map/ppermute | solution.py:243
  69.7 2.7 %collective-permute-done.12.refs_5_ = bf16[128,512]{1,0:T(8,128)(2,1)S(1)} collective-permute-done((bf16[128,512]{1,0:T(8,128)(2,1)S(1)}, bf16[128,512]{1,0:T(8,128)(2,1)S(1)}, u32[]{:S(2)}, u32[]{:S(2)}) %collective-permute-start.12) | collective-permute-done | bytes 131104 | tf_op jit(solution)/shard_map/ppermute | solution.py:272
  72.4 0.3 shard_map.101.refs_2_
  72.7 0.0 all-to-all-done.refs_0_
  72.7 0.0 copy-done
  72.7 1.3 %shard_map.102 = bf16[256,256]{1,0:T(8,128)(2,1)S(1)} custom-call(bf16[8,64,512]{2,1,0:T(8,128)(2,1)S(1)} %all-to-all-done.refs_0_, bf16[1,1024,512]{2,1,0:T(8,128)(2,1)S(1)} %copy-done, f32[256,256]{1,0:T(8,128)S(1)} %shard_map.101.refs_2_, bf16[256,256]{1,0:T(8,128)(2,1)S(1)} %get-tuple-element.19.refs_3_), custom_call_target="tpu_custom_call" | custom-call | flops 1048576 | bytes 1048576 | tf_op jit(solution)/shard_map/pallas_call | solution.py:34
  74.1 11.3 %all_to_all.10.refs_0_ = bf16[8,32,256]{2,1,0:T(8,128)(2,1)S(1)} all-to-all(bf16[8,32,256]{2,1,0:T(8,128)(2,1)S(1)} %bitcast.2), channel_id=1, replica_groups=mesh['xh'=2,'z'=8,'core'=2,'xl'=2,'y'=4] {'xl','y'}, dimensions={0} | all-to-all | bytes 262144 | tf_op jit(solution)/shard_map/all_to_all | solution.py:279
  85.4 0.8 shard_map.103
  (5 shorter events, 0.0 us)
Async XLA Ops:
  1.9 1.6 %collective-permute-start = (bf16[4,64,512]{2,1,0:T(8,128)(2,1)S(1)}, bf16[4,64,512]{2,1,0:T(8,128)(2,1)S(1)}, u32[]{:S(2)}, u32[]{:S(2)}) collective-permute-start(bf16[4,64,512]{2,1,0:T(8,128)(2,1)S(1)} %get-tuple-element.16), channel_id=1, source_target_pairs={{0,8},{8,0},{1,9},{9,1},{2,10},{10,2},{3,11},{11,3},{4,12},{12,4},... | collective-permute-start | bytes 786440 | tf_op jit(solution)/shard_map/ppermute | solution.py:243
  4.4 5.8 %collective-permute-start.1 = (bf16[8,64,512]{2,1,0:T(8,128)(2,1)S(1)}, bf16[8,64,512]{2,1,0:T(8,128)(2,1)S(1)}, u32[]{:S(2)}, u32[]{:S(2)}) collective-permute-start(bf16[8,64,512]{2,1,0:T(8,128)(2,1)S(1)} %shard_map.93), channel_id=1, source_target_pairs={{0,8},{8,0},{1,9},{9,1},{2,10},{10,2},{3,11},{11,3},{4,12},{12,4},... | collective-permute-start | bytes 1572872 | tf_op jit(solution)/shard_map/ppermute | solution.py:243
  4.6 3.4 %collective-permute-start.3 = (bf16[4,64,512]{2,1,0:T(8,128)(2,1)S(1)}, bf16[4,64,512]{2,1,0:T(8,128)(2,1)S(1)}, u32[]{:S(2)}, u32[]{:S(2)}) collective-permute-start(bf16[4,64,512]{2,1,0:T(8,128)(2,1)S(1)} %get-tuple-element.17), channel_id=1, source_target_pairs={{0,8},{8,0},{1,9},{9,1},{2,10},{10,2},{3,11},{11,3},{4,12},{12,4},... | collective-permute-start | bytes 786440 | tf_op jit(solution)/shard_map/ppermute | solution.py:243
  5.0 10.7 %collective-permute-start.2 = (bf16[4,64,512]{2,1,0:T(8,128)(2,1)S(1)}, bf16[4,64,512]{2,1,0:T(8,128)(2,1)S(1)}, u32[]{:S(2)}, u32[]{:S(2)}) collective-permute-start(bf16[4,64,512]{2,1,0:T(8,128)(2,1)S(1)} %shard_map.92.refs_3_.refs_4_), channel_id=1, source_target_pairs={{0,128},{128,0},{1,129},{129,1},{2,130},{130,2},{3,131},{131,3},{4... | collective-permute-start | bytes 786440 | tf_op jit(solution)/shard_map/ppermute | solution.py:243
  8.3 12.1 %collective-permute-start.4 = (bf16[4,64,512]{2,1,0:T(8,128)(2,1)S(1)}, bf16[4,64,512]{2,1,0:T(8,128)(2,1)S(1)}, u32[]{:S(2)}, u32[]{:S(2)}) collective-permute-start(bf16[4,64,512]{2,1,0:T(8,128)(2,1)S(1)} %shard_map.95), channel_id=1, source_target_pairs={{0,128},{128,0},{1,129},{129,1},{2,130},{130,2},{3,131},{131,3},{4... | collective-permute-start | bytes 786440 | tf_op jit(solution)/shard_map/ppermute | solution.py:243
  21.3 8.7 %copy-start.1 = (bf16[1,256,512]{2,1,0:T(8,128)(2,1)S(1)}, bf16[1,256,512]{2,1,0:T(8,128)(2,1)}, u32[]{:S(2)}) copy-start(bf16[1,256,512]{2,1,0:T(8,128)(2,1)} %refs_1_.6) | copy-start | bytes 786436
  21.3 51.4 %all-to-all-start = ((bf16[8,64,512]{2,1,0:T(8,128)(2,1)}), bf16[8,64,512]{2,1,0:T(8,128)(2,1)S(1)}, u32[]{:S(2)}, u32[]{:S(2)}) async-start(bf16[8,64,512]{2,1,0:T(8,128)(2,1)} %shard_map.96), calls=%async_computation | async-start | bytes 1048576 | tf_op jit(solution)/shard_map/all_to_all | solution.py:275
  30.0 1.5 %collective-permute-start.5 = (bf16[1,256,512]{2,1,0:T(8,128)(2,1)S(1)}, bf16[1,256,512]{2,1,0:T(8,128)(2,1)S(1)}, u32[]{:S(2)}, u32[]{:S(2)}) collective-permute-start(bf16[1,256,512]{2,1,0:T(8,128)(2,1)S(1)} %copy-done.1), channel_id=1, source_target_pairs={{0,8},{8,0},{1,9},{9,1},{2,10},{10,2},{3,11},{11,3},{4,12},{12,4},... | collective-permute-start | bytes 786440 | tf_op jit(solution)/shard_map/ppermute | solution.py:243
  31.6 12.2 %collective-permute-start.6 = (bf16[128,512]{1,0:T(8,128)(2,1)S(1)}, bf16[128,512]{1,0:T(8,128)(2,1)S(1)}, u32[]{:S(2)}, u32[]{:S(2)}) collective-permute-start(bf16[128,512]{1,0:T(8,128)(2,1)S(1)} %shard_map.98.refs_1_), channel_id=1, source_target_pairs={{0,16},{16,32},{32,48},{48,64},{64,80},{80,96},{96,112},{112,0},{1... | collective-permute-start | bytes 393224 | tf_op jit(solution)/shard_map/ppermute | solution.py:243
  33.1 11.2 %collective-permute-start.7 = (bf16[128,512]{1,0:T(8,128)(2,1)S(1)}, bf16[128,512]{1,0:T(8,128)(2,1)S(1)}, u32[]{:S(2)}, u32[]{:S(2)}) collective-permute-start(bf16[128,512]{1,0:T(8,128)(2,1)S(1)} %shard_map.98.refs_1_), channel_id=1, source_target_pairs={{0,112},{16,0},{32,16},{48,32},{64,48},{80,64},{96,80},{112,96},{1... | collective-permute-start | bytes 393224 | tf_op jit(solution)/shard_map/ppermute | solution.py:243
  44.3 21.4 %copy-start.4 = (bf16[512]{0:T(512)(128)(2,1)S(1)}, bf16[512]{0:T(512)(128)(2,1)}, u32[]{:S(2)}) copy-start(bf16[512]{0:T(512)(128)(2,1)} %param.13) | copy-start | bytes 3076
  44.3 21.4 %copy-start.2 = (s32[32,256]{1,0:T(8,128)S(1)}, s32[32,256]{1,0:T(8,128)}, u32[]{:S(2)}) copy-start(s32[32,256]{1,0:T(8,128)} %refs_2_.3) | copy-start | bytes 98308
  44.3 21.4 %copy-start.3 = (s32[32]{0:T(128)S(1)}, s32[32]{0:T(128)}, u32[]{:S(2)}) copy-start(s32[32]{0:T(128)} %refs_1_.5) | copy-start | bytes 388
  44.3 28.4 %copy-start = (bf16[1,1024,512]{2,1,0:T(8,128)(2,1)S(1)}, bf16[1,1024,512]{2,1,0:T(8,128)(2,1)}, u32[]{:S(2)}) copy-start(bf16[1,1024,512]{2,1,0:T(8,128)(2,1)} %refs_1_.7) | copy-start | bytes 3145732
  44.3 12.6 %collective-permute-start.8 = (bf16[128,512]{1,0:T(8,128)(2,1)S(1)}, bf16[128,512]{1,0:T(8,128)(2,1)S(1)}, u32[]{:S(2)}, u32[]{:S(2)}) collective-permute-start(bf16[128,512]{1,0:T(8,128)(2,1)S(1)} %shard_map.99.refs_1_), channel_id=1, source_target_pairs={{0,48},{16,64},{32,80},{48,96},{64,112},{80,0},{96,16},{112,32},{1... | collective-permute-start | bytes 393224 | tf_op jit(solution)/shard_map/ppermute | solution.py:243
  49.0 13.2 %collective-permute-start.9 = (bf16[128,512]{1,0:T(8,128)(2,1)S(1)}, bf16[128,512]{1,0:T(8,128)(2,1)S(1)}, u32[]{:S(2)}, u32[]{:S(2)}) collective-permute-start(bf16[128,512]{1,0:T(8,128)(2,1)S(1)} %shard_map.99.refs_1_), channel_id=1, source_target_pairs={{0,80},{16,96},{32,112},{48,0},{64,16},{80,32},{96,48},{112,64},{1... | collective-permute-start | bytes 393224 | tf_op jit(solution)/shard_map/ppermute | solution.py:243
  62.2 4.2 %collective-permute-start.10 = (bf16[128,512]{1,0:T(8,128)(2,1)S(1)}, bf16[128,512]{1,0:T(8,128)(2,1)S(1)}, u32[]{:S(2)}, u32[]{:S(2)}) collective-permute-start(bf16[128,512]{1,0:T(8,128)(2,1)S(1)} %shard_map.100.refs_2_), channel_id=1, source_target_pairs={{0,8},{8,0},{1,9},{9,1},{2,10},{10,2},{3,11},{11,3},{4,12},{12,4},... | collective-permute-start | bytes 393224 | tf_op jit(solution)/shard_map/ppermute | solution.py:243
  62.3 7.4 %collective-permute-start.11 = (bf16[128,512]{1,0:T(8,128)(2,1)S(1)}, bf16[128,512]{1,0:T(8,128)(2,1)S(1)}, u32[]{:S(2)}, u32[]{:S(2)}) collective-permute-start(bf16[128,512]{1,0:T(8,128)(2,1)S(1)} %shard_map.100.refs_2_), channel_id=1, source_target_pairs={{0,128},{128,0},{1,129},{129,1},{2,130},{130,2},{3,131},{131,3},{4... | collective-permute-start | bytes 393224 | tf_op jit(solution)/shard_map/ppermute | solution.py:243
  65.4 7.0 %collective-permute-start.12 = (bf16[128,512]{1,0:T(8,128)(2,1)S(1)}, bf16[128,512]{1,0:T(8,128)(2,1)S(1)}, u32[]{:S(2)}, u32[]{:S(2)}) collective-permute-start(bf16[128,512]{1,0:T(8,128)(2,1)S(1)} %shard_map.100.refs_2_), channel_id=1, source_target_pairs={{0,136},{8,128},{128,8},{136,0},{1,137},{9,129},{129,9},{137,1},{2... | collective-permute-start | bytes 393224 | tf_op jit(solution)/shard_map/ppermute | solution.py:272

commit v4 on v3

--- a/solution.py
+++ b/solution.py
@@ -56,33 +56,30 @@
         emit(z, dot(val_ref[k], w_ref[q_ref[k]]))
 
 
-def to_other_core(q_index, val, screened, after=()):
+def to_other_core(other_x, group, q_index, val, screened, after=()):
     def body(q_ref, val_ref, w_ref, out_ref):
         def emit(z, r):
-            out_ref[z] = r.astype(BF)
-
-        partial_terms((q_ref, val_ref, w_ref), False, True, emit)
-
-    return call(body, pltpu.VMEM((Z, val.shape[1], screened.shape[1]), BF), [q_index], [val, screened], after)
-
-
-def first_terms(q_index, val, screened):
-    half = Z // 2
-
-    def body(q_ref, val_ref, w_ref, low_ref, high_ref, val_out, w_out, q_out):
-        def emit(z, r):
-            (low_ref if z < half else high_ref)[z % half] = r.astype(BF)
+            out_ref[z - group[0]] = r.astype(BF)
+
+        partial_terms((q_ref, val_ref, w_ref), other_x, True, emit, group)
+
+    out = pltpu.VMEM((len(group), val.shape[1], screened.shape[1]), BF)
+    return call(body, out, [q_index], [val, screened], after)
+
+
+def first_terms(group, q_index, val, screened):
+    def body(q_ref, val_ref, w_ref, out_ref, val_out, w_out, q_out):
+        def emit(z, r):
+            out_ref[z - group[0]] = r.astype(BF)
 
         for k in range(q_ref.shape[0]):
             q_out[k] = q_ref[k]
-
-        partial_terms((q_ref, val_ref, w_ref), True, True, emit)
+        partial_terms((q_ref, val_ref, w_ref), True, True, emit, group)
         val_out[...] = val_ref[...]
         w_out[...] = w_ref[...]
 
     out = (
-        pltpu.VMEM((half, val.shape[1], screened.shape[1]), BF),
-        pltpu.VMEM((half, val.shape[1], screened.shape[1]), BF),
+        pltpu.VMEM((len(group), val.shape[1], screened.shape[1]), BF),
         pltpu.VMEM(val.shape, BF),
         pltpu.VMEM(screened.shape, BF),
         pltpu.SMEM(q_index.shape, jnp.int32),
@@ -150,25 +147,25 @@
     return call(body, pltpu.VMEM((half, own.shape[2]), BF), [column], [own, sib])
 
 
-def pick(column, own, below, above, reach, after=()):
+def pick(column, own, below, above, low, high):
     def body(c_ref, own_ref, below_ref, above_ref, out_ref):
         d = (lax.axis_index("z") - (c_ref[0] // CORE) % Z + Z) % Z
-        low = (d > reach) & (d <= Z // 2) if reach else d == 1
-        high = (d > Z // 2) & (d < Z - reach) if reach else d == Z - 1
-
-        @pl.when(low)
+        from_below = (d >= low[0]) & (d <= low[1])
+        from_above = (d >= high[0]) & (d <= high[1])
+
+        @pl.when(from_below)
         def _():
             out_ref[...] = below_ref[...]
 
-        @pl.when(high)
+        @pl.when(from_above)
         def _():
             out_ref[...] = above_ref[...]
 
-        @pl.when(jnp.logical_not(low | high))
+        @pl.when(jnp.logical_not(from_below | from_above))
         def _():
             out_ref[...] = own_ref[...]
 
-    return call(body, pltpu.VMEM(own.shape, BF), [column], [own, below, above], after)
+    return call(body, pltpu.VMEM(own.shape, BF), [column], [own, below, above])
 
 
 def add(own, low, high):
@@ -252,22 +249,24 @@
 ):
     slots = pair_dens.shape[1]
     sib = swap(pair_dens, "core")
-    low, high, val_near, screened_near, q_index = first_terms(q_index, val_dens, screened)
+    groups = range(Z // 2), range(Z // 2, Z)
+    low, val_near, screened_near, q_index = first_terms(groups[0], q_index, val_dens, screened)
+    high = to_other_core(True, groups[1], q_index, val_near, screened_near)
     low = swap(low, "core")
     high = swap(high, "core")
-    low = low_terms = to_other_x(q_index, val_near, screened_near, near(low), 0)
-    high = to_other_x(q_index, val_near, screened_near, near(high), 1, (low,))
+    low = to_other_x(q_index, val_near, screened_near, near(low), 0)
+    high = high_terms = to_other_x(q_index, val_near, screened_near, near(high), 1, (low,))
     low = swap(low, "xh")
     high = swap(high, "xh")
-    to_core = to_other_core(q_index, val_near, screened_near, (low_terms,))
+    to_core = to_other_core(False, range(Z), q_index, val_near, screened_near, (high_terms,))
     from_core_2 = swap(to_core, "core")
     own = own_terms(q_index, val_near, screened_near, near(from_core_2))
     weighted, pt, ps = prepare(column_k, counts, pair_list, pair_dens, coulomb)
     half = half_of_column(column_k, near(pair_dens), near(sib))
     ups, downs = (shift(half, "z", Z, by) for by in (1, -1))
-    once = pick(column_k, half, near(ups), near(downs), 0)
-    ups, downs = (shift(once, "z", Z, by) for by in (3, -3))
-    own_half = pick(column_k, once, near(ups), near(downs), 1)
+    once = pick(column_k, half, near(ups), near(downs), (1, 1), (Z - 1, Z - 1))
+    ups, downs = (shift(once, "z", Z, by) for by in (3, -2))
+    own_half = pick(column_k, once, near(ups), near(downs), (2, 4), (5, 6))
     own_x = swap(own_half, "xh")
     sib_x = lax.ppermute(own_half, ("xh", "core"), [(i, 3 - i) for i in range(4)])
     sib_half = swap(own_half, "core")

time: 86.4 us -> 83 us (0.961)
  the two profiles are of different devices: /device:TPU:32 before, /device:TPU:2 now
where the time goes in v4:
time: 83 us; the launch traced here: 82 us
  waiting for transfers between devices  38.8 us (47%)
  starting transfers between devices  23.7 us (29%)
  blocking collectives  11 us (13%)
  Pallas kernels  7.66 us (9%)
    ppermute x12, waiting for transfers between devices, shift(): return lax.ppermute(x, axis, [(i, (i + by) % size) for i in range(size)])  37.1 us
    ppermute x12, starting transfers between devices, shift(): return lax.ppermute(x, axis, [(i, (i + by) % size) for i in range(size)])  14 us
    all_to_all x1, blocking collectives, per_device(): lax.all_to_all(combined.reshape(XL * Y, -1, slots), GA, 0, 0, tiled=True)  11 us
    all_to_all x1, starting transfers between devices, per_device(): arrived = lax.all_to_all(to_z, 'z', 0, 0, tiled=True)  8.6 us
    pallas_call x14, Pallas kernels, call(): pl.pallas_call(run, out_shape=out, in_specs=[SMEM] * len(scalars) + [VMEM...  7.66 us
    ppermute x1, waiting for transfers between devices, per_device(): lax.ppermute(own_half, ('xh', 'core'), [(i, 3 - i) for i in range(4)])  1.68 us
  transfers between devices with their start and end apart: 14, of which 9 were waited for; matrix products, arithmetic and copies ran while one was open for 0% of the time, Pallas kernels for 3%

profile of v4, /device:TPU:2, one launch (start us, length us, event | category | flops | bytes accessed | tf_op | source)
XLA Modules:
  0.0 82.0 jit_solution(936785402491069033)
XLA Ops:
  0.0 1.8 %shard_map.91 = (bf16[4,64,512]{2,1,0:T(8,128)(2,1)S(1)}, bf16[32,64,128]{2,1,0:T(8,128)(2,1)S(1)}, bf16[8,512,128]{2,1,0:T(8,128)(2,1)S(1)}, s32[32]{0:T(128)S(4)}) custom-call(s32[32]{0:T(128)} %refs_0_.6, bf16[32,64,128]{2,1,0:T(8,128)(2,1)} %refs_1_.4, bf16[8,512,128]{2,1,0:T(8,128)(2,1)} %refs_2_.2), custom_call_target="tpu_custom_call" | custom-call | flops 1048576 | bytes 1048576 | tf_op jit(solution)/shard_map/pallas_call | solution.py:34
  1.8 0.1 collective-permute-start.1
  1.9 0.3 shard_map.92
  2.2 0.6 collective-permute-start
  2.7 0.6 collective-permute-done.1.refs_3_
  3.4 0.3 shard_map.93.refs_4_
  3.7 0.2 collective-permute-done.refs_3_
  3.9 0.3 shard_map.94.refs_3_
  4.2 0.5 shard_map.95
  4.7 0.5 collective-permute-start.2
  5.2 2.1 %collective-permute-start.3 = (bf16[4,64,512]{2,1,0:T(8,128)(2,1)S(1)}, bf16[4,64,512]{2,1,0:T(8,128)(2,1)S(1)}, u32[]{:S(2)}, u32[]{:S(2)}) collective-permute-start(bf16[4,64,512]{2,1,0:T(8,128)(2,1)S(1)} %shard_map.93.refs_4_), channel_id=1, source_target_pairs={{0,128},{128,0},{1,129},{129,1},{2,130},{130,2},{3,131},{131,3},{4... | collective-permute-start | bytes 786440 | tf_op jit(solution)/shard_map/ppermute | solution.py:240
  7.3 1.4 %collective-permute-start.4 = (bf16[4,64,512]{2,1,0:T(8,128)(2,1)S(1)}, bf16[4,64,512]{2,1,0:T(8,128)(2,1)S(1)}, u32[]{:S(2)}, u32[]{:S(2)}) collective-permute-start(bf16[4,64,512]{2,1,0:T(8,128)(2,1)S(1)} %shard_map.94.refs_3_), channel_id=1, source_target_pairs={{0,128},{128,0},{1,129},{129,1},{2,130},{130,2},{3,131},{131,3},{4... | collective-permute-start | bytes 786440 | tf_op jit(solution)/shard_map/ppermute | solution.py:240
  8.7 0.0 collective-permute-done.2.refs_3_
  8.7 0.5 shard_map.96.refs_0_
  9.2 6.7 %collective-permute-done.3.refs_1_ = bf16[4,64,512]{2,1,0:T(8,128)(2,1)S(1)} collective-permute-done((bf16[4,64,512]{2,1,0:T(8,128)(2,1)S(1)}, bf16[4,64,512]{2,1,0:T(8,128)(2,1)S(1)}, u32[]{:S(2)}, u32[]{:S(2)}) %collective-permute-start.3) | collective-permute-done | bytes 262176 | tf_op jit(solution)/shard_map/ppermute | solution.py:240
  15.9 4.8 %collective-permute-done.4.refs_2_ = bf16[4,64,512]{2,1,0:T(8,128)(2,1)S(1)} collective-permute-done((bf16[4,64,512]{2,1,0:T(8,128)(2,1)S(1)}, bf16[4,64,512]{2,1,0:T(8,128)(2,1)S(1)}, u32[]{:S(2)}, u32[]{:S(2)}) %collective-permute-start.4) | collective-permute-done | bytes 262176 | tf_op jit(solution)/shard_map/ppermute | solution.py:240
  20.6 0.9 %shard_map.97 = bf16[8,64,512]{2,1,0:T(8,128)(2,1)} custom-call(f32[8,64,512]{2,1,0:T(8,128)S(1)} %shard_map.96.refs_0_, bf16[4,64,512]{2,1,0:T(8,128)(2,1)S(1)} %collective-permute-done.3.refs_1_, bf16[4,64,512]{2,1,0:T(8,128)(2,1)S(1)} %collective-permute-done.4.refs_2_), custom_call_target="tpu_custom_call" | custom-call | flops 1048576 | bytes 1048576 | tf_op jit(solution)/shard_map/pallas_call | solution.py:34
  21.5 0.0 copy-start.1
  21.5 8.6 %all-to-all-start = ((bf16[8,64,512]{2,1,0:T(8,128)(2,1)}), bf16[8,64,512]{2,1,0:T(8,128)(2,1)S(1)}, u32[]{:S(2)}, u32[]{:S(2)}) async-start(bf16[8,64,512]{2,1,0:T(8,128)(2,1)} %shard_map.97), calls=%async_computation | async-start | bytes 1048576 | tf_op jit(solution)/shard_map/all_to_all | solution.py:274
  30.1 0.0 copy-done.1
  30.1 0.1 collective-permute-start.5
  30.9 0.9 %collective-permute-done.5.refs_2_ = bf16[1,256,512]{2,1,0:T(8,128)(2,1)S(1)} collective-permute-done((bf16[1,256,512]{2,1,0:T(8,128)(2,1)S(1)}, bf16[1,256,512]{2,1,0:T(8,128)(2,1)S(1)}, u32[]{:S(2)}, u32[]{:S(2)}) %collective-permute-start.5) | collective-permute-done | bytes 262176 | tf_op jit(solution)/shard_map/ppermute | solution.py:240
  31.8 2.0 %collective-permute-start.6 = (bf16[128,512]{1,0:T(8,128)(2,1)S(1)}, bf16[128,512]{1,0:T(8,128)(2,1)S(1)}, u32[]{:S(2)}, u32[]{:S(2)}) collective-permute-start(bf16[128,512]{1,0:T(8,128)(2,1)S(1)} %shard_map.99.refs_1_), channel_id=1, source_target_pairs={{0,16},{16,32},{32,48},{48,64},{64,80},{80,96},{96,112},{112,0},{1... | collective-permute-start | bytes 393224 | tf_op jit(solution)/shard_map/ppermute | solution.py:240
  33.8 1.3 %collective-permute-start.7 = (bf16[128,512]{1,0:T(8,128)(2,1)S(1)}, bf16[128,512]{1,0:T(8,128)(2,1)S(1)}, u32[]{:S(2)}, u32[]{:S(2)}) collective-permute-start(bf16[128,512]{1,0:T(8,128)(2,1)S(1)} %shard_map.99.refs_1_), channel_id=1, source_target_pairs={{0,112},{16,0},{32,16},{48,32},{64,48},{80,64},{96,80},{112,96},{1... | collective-permute-start | bytes 393224 | tf_op jit(solution)/shard_map/ppermute | solution.py:240
  35.1 11.8 %collective-permute-done.6.refs_2_ = bf16[128,512]{1,0:T(8,128)(2,1)S(1)} collective-permute-done((bf16[128,512]{1,0:T(8,128)(2,1)S(1)}, bf16[128,512]{1,0:T(8,128)(2,1)S(1)}, u32[]{:S(2)}, u32[]{:S(2)}) %collective-permute-start.6) | collective-permute-done | bytes 131104 | tf_op jit(solution)/shard_map/ppermute | solution.py:240
  46.9 0.0 collective-permute-done.7.refs_3_
  46.9 0.0 copy-start.4
  46.9 0.0 copy-start
  46.9 3.6 %collective-permute-start.8 = (bf16[128,512]{1,0:T(8,128)(2,1)S(1)}, bf16[128,512]{1,0:T(8,128)(2,1)S(1)}, u32[]{:S(2)}, u32[]{:S(2)}) collective-permute-start(bf16[128,512]{1,0:T(8,128)(2,1)S(1)} %shard_map.100.refs_1_), channel_id=1, source_target_pairs={{0,48},{16,64},{32,80},{48,96},{64,112},{80,0},{96,16},{112,32},{1... | collective-permute-start | bytes 393224 | tf_op jit(solution)/shard_map/ppermute | solution.py:240
  50.6 0.0 collective-permute-start.9
  50.6 8.3 %collective-permute-done.8.refs_2_ = bf16[128,512]{1,0:T(8,128)(2,1)S(1)} collective-permute-done((bf16[128,512]{1,0:T(8,128)(2,1)S(1)}, bf16[128,512]{1,0:T(8,128)(2,1)S(1)}, u32[]{:S(2)}, u32[]{:S(2)}) %collective-permute-start.8) | collective-permute-done | bytes 131104 | tf_op jit(solution)/shard_map/ppermute | solution.py:240
  58.8 0.0 collective-permute-done.9.refs_3_
  58.8 0.1 collective-permute-start.10
  58.9 2.2 %collective-permute-start.11 = (bf16[128,512]{1,0:T(8,128)(2,1)S(1)}, bf16[128,512]{1,0:T(8,128)(2,1)S(1)}, u32[]{:S(2)}, u32[]{:S(2)}) collective-permute-start(bf16[128,512]{1,0:T(8,128)(2,1)S(1)} %shard_map.101.refs_2_), channel_id=1, source_target_pairs={{0,128},{128,0},{1,129},{129,1},{2,130},{130,2},{3,131},{131,3},{4... | collective-permute-start | bytes 393224 | tf_op jit(solution)/shard_map/ppermute | solution.py:240
  61.2 1.1 %collective-permute-start.12 = (bf16[128,512]{1,0:T(8,128)(2,1)S(1)}, bf16[128,512]{1,0:T(8,128)(2,1)S(1)}, u32[]{:S(2)}, u32[]{:S(2)}) collective-permute-start(bf16[128,512]{1,0:T(8,128)(2,1)S(1)} %shard_map.101.refs_2_), channel_id=1, source_target_pairs={{0,136},{8,128},{128,8},{136,0},{1,137},{9,129},{129,9},{137,1},{2... | collective-permute-start | bytes 393224 | tf_op jit(solution)/shard_map/ppermute | solution.py:271
  62.3 0.0 copy-done.4
  62.3 0.0 copy-done.2
  62.3 0.0 copy-done.3
  62.3 0.7 shard_map.98
  63.0 0.0 collective-permute-done.10.refs_3_
  63.0 3.9 %collective-permute-done.11.refs_4_ = bf16[128,512]{1,0:T(8,128)(2,1)S(1)} collective-permute-done((bf16[128,512]{1,0:T(8,128)(2,1)S(1)}, bf16[128,512]{1,0:T(8,128)(2,1)S(1)}, u32[]{:S(2)}, u32[]{:S(2)}) %collective-permute-start.11) | collective-permute-done | bytes 131104 | tf_op jit(solution)/shard_map/ppermute | solution.py:240
  66.9 1.7 %collective-permute-done.12.refs_5_ = bf16[128,512]{1,0:T(8,128)(2,1)S(1)} collective-permute-done((bf16[128,512]{1,0:T(8,128)(2,1)S(1)}, bf16[128,512]{1,0:T(8,128)(2,1)S(1)}, u32[]{:S(2)}, u32[]{:S(2)}) %collective-permute-start.12) | collective-permute-done | bytes 131104 | tf_op jit(solution)/shard_map/ppermute | solution.py:271
  68.6 0.3 shard_map.102.refs_2_
  68.9 0.0 all-to-all-done.refs_0_
  68.9 0.0 copy-done
  68.9 1.3 %shard_map.103 = bf16[256,256]{1,0:T(8,128)(2,1)S(1)} custom-call(bf16[8,64,512]{2,1,0:T(8,128)(2,1)S(1)} %all-to-all-done.refs_0_, bf16[1,1024,512]{2,1,0:T(8,128)(2,1)S(1)} %copy-done, f32[256,256]{1,0:T(8,128)S(1)} %shard_map.102.refs_2_, bf16[256,256]{1,0:T(8,128)(2,1)S(1)} %get-tuple-element.17.refs_3_), custom_call_target="tpu_custom_call" | custom-call | flops 1048576 | bytes 1048576 | tf_op jit(solution)/shard_map/pallas_call | solution.py:34
  70.2 11.0 %all_to_all.10.refs_0_ = bf16[8,32,256]{2,1,0:T(8,128)(2,1)S(1)} all-to-all(bf16[8,32,256]{2,1,0:T(8,128)(2,1)S(1)} %bitcast.2), channel_id=1, replica_groups=mesh['xh'=2,'z'=8,'core'=2,'xl'=2,'y'=4] {'xl','y'}, dimensions={0} | all-to-all | bytes 262144 | tf_op jit(solution)/shard_map/all_to_all | solution.py:278
  81.2 0.8 shard_map.104
  (6 shorter events, 0.1 us)
Async XLA Ops:
  1.8 1.6 %collective-permute-start.1 = (bf16[4,64,512]{2,1,0:T(8,128)(2,1)S(1)}, bf16[4,64,512]{2,1,0:T(8,128)(2,1)S(1)}, u32[]{:S(2)}, u32[]{:S(2)}) collective-permute-start(bf16[4,64,512]{2,1,0:T(8,128)(2,1)S(1)} %get-tuple-element.15), channel_id=1, source_target_pairs={{0,8},{8,0},{1,9},{9,1},{2,10},{10,2},{3,11},{11,3},{4,12},{12,4},... | collective-permute-start | bytes 786440 | tf_op jit(solution)/shard_map/ppermute | solution.py:240
  2.2 1.7 %collective-permute-start = (bf16[4,64,512]{2,1,0:T(8,128)(2,1)S(1)}, bf16[4,64,512]{2,1,0:T(8,128)(2,1)S(1)}, u32[]{:S(2)}, u32[]{:S(2)}) collective-permute-start(bf16[4,64,512]{2,1,0:T(8,128)(2,1)S(1)} %shard_map.92), channel_id=1, source_target_pairs={{0,8},{8,0},{1,9},{9,1},{2,10},{10,2},{3,11},{11,3},{4,12},{12,4},... | collective-permute-start | bytes 786440 | tf_op jit(solution)/shard_map/ppermute | solution.py:240
  4.7 4.0 %collective-permute-start.2 = (bf16[8,64,512]{2,1,0:T(8,128)(2,1)S(1)}, bf16[8,64,512]{2,1,0:T(8,128)(2,1)S(1)}, u32[]{:S(2)}, u32[]{:S(2)}) collective-permute-start(bf16[8,64,512]{2,1,0:T(8,128)(2,1)S(1)} %shard_map.95), channel_id=1, source_target_pairs={{0,8},{8,0},{1,9},{9,1},{2,10},{10,2},{3,11},{11,3},{4,12},{12,4},... | collective-permute-start | bytes 1572872 | tf_op jit(solution)/shard_map/ppermute | solution.py:240
  5.2 10.7 %collective-permute-start.3 = (bf16[4,64,512]{2,1,0:T(8,128)(2,1)S(1)}, bf16[4,64,512]{2,1,0:T(8,128)(2,1)S(1)}, u32[]{:S(2)}, u32[]{:S(2)}) collective-permute-start(bf16[4,64,512]{2,1,0:T(8,128)(2,1)S(1)} %shard_map.93.refs_4_), channel_id=1, source_target_pairs={{0,128},{128,0},{1,129},{129,1},{2,130},{130,2},{3,131},{131,3},{4... | collective-permute-start | bytes 786440 | tf_op jit(solution)/shard_map/ppermute | solution.py:240
  7.3 13.3 %collective-permute-start.4 = (bf16[4,64,512]{2,1,0:T(8,128)(2,1)S(1)}, bf16[4,64,512]{2,1,0:T(8,128)(2,1)S(1)}, u32[]{:S(2)}, u32[]{:S(2)}) collective-permute-start(bf16[4,64,512]{2,1,0:T(8,128)(2,1)S(1)} %shard_map.94.refs_3_), channel_id=1, source_target_pairs={{0,128},{128,0},{1,129},{129,1},{2,130},{130,2},{3,131},{131,3},{4... | collective-permute-start | bytes 786440 | tf_op jit(solution)/shard_map/ppermute | solution.py:240
  21.5 8.6 %copy-start.1 = (bf16[1,256,512]{2,1,0:T(8,128)(2,1)S(1)}, bf16[1,256,512]{2,1,0:T(8,128)(2,1)}, u32[]{:S(2)}) copy-start(bf16[1,256,512]{2,1,0:T(8,128)(2,1)} %refs_1_.6) | copy-start | bytes 786436
  21.5 47.3 %all-to-all-start = ((bf16[8,64,512]{2,1,0:T(8,128)(2,1)}), bf16[8,64,512]{2,1,0:T(8,128)(2,1)S(1)}, u32[]{:S(2)}, u32[]{:S(2)}) async-start(bf16[8,64,512]{2,1,0:T(8,128)(2,1)} %shard_map.97), calls=%async_computation | async-start | bytes 1048576 | tf_op jit(solution)/shard_map/all_to_all | solution.py:274
  30.1 1.6 %collective-permute-start.5 = (bf16[1,256,512]{2,1,0:T(8,128)(2,1)S(1)}, bf16[1,256,512]{2,1,0:T(8,128)(2,1)S(1)}, u32[]{:S(2)}, u32[]{:S(2)}) collective-permute-start(bf16[1,256,512]{2,1,0:T(8,128)(2,1)S(1)} %copy-done.1), channel_id=1, source_target_pairs={{0,8},{8,0},{1,9},{9,1},{2,10},{10,2},{3,11},{11,3},{4,12},{12,4},... | collective-permute-start | bytes 786440 | tf_op jit(solution)/shard_map/ppermute | solution.py:240
  31.8 15.1 %collective-permute-start.6 = (bf16[128,512]{1,0:T(8,128)(2,1)S(1)}, bf16[128,512]{1,0:T(8,128)(2,1)S(1)}, u32[]{:S(2)}, u32[]{:S(2)}) collective-permute-start(bf16[128,512]{1,0:T(8,128)(2,1)S(1)} %shard_map.99.refs_1_), channel_id=1, source_target_pairs={{0,16},{16,32},{32,48},{48,64},{64,80},{80,96},{96,112},{112,0},{1... | collective-permute-start | bytes 393224 | tf_op jit(solution)/shard_map/ppermute | solution.py:240
  33.8 13.1 %collective-permute-start.7 = (bf16[128,512]{1,0:T(8,128)(2,1)S(1)}, bf16[128,512]{1,0:T(8,128)(2,1)S(1)}, u32[]{:S(2)}, u32[]{:S(2)}) collective-permute-start(bf16[128,512]{1,0:T(8,128)(2,1)S(1)} %shard_map.99.refs_1_), channel_id=1, source_target_pairs={{0,112},{16,0},{32,16},{48,32},{64,48},{80,64},{96,80},{112,96},{1... | collective-permute-start | bytes 393224 | tf_op jit(solution)/shard_map/ppermute | solution.py:240
  46.9 15.4 %copy-start.4 = (bf16[512]{0:T(512)(128)(2,1)S(1)}, bf16[512]{0:T(512)(128)(2,1)}, u32[]{:S(2)}) copy-start(bf16[512]{0:T(512)(128)(2,1)} %param.13) | copy-start | bytes 3076
  46.9 15.4 %copy-start.2 = (s32[32,256]{1,0:T(8,128)S(1)}, s32[32,256]{1,0:T(8,128)}, u32[]{:S(2)}) copy-start(s32[32,256]{1,0:T(8,128)} %refs_2_.3) | copy-start | bytes 98308
  46.9 15.4 %copy-start.3 = (s32[32]{0:T(128)S(1)}, s32[32]{0:T(128)}, u32[]{:S(2)}) copy-start(s32[32]{0:T(128)} %refs_1_.5) | copy-start | bytes 388
  46.9 22.0 %copy-start = (bf16[1,1024,512]{2,1,0:T(8,128)(2,1)S(1)}, bf16[1,1024,512]{2,1,0:T(8,128)(2,1)}, u32[]{:S(2)}) copy-start(bf16[1,1024,512]{2,1,0:T(8,128)(2,1)} %refs_1_.7) | copy-start | bytes 3145732
  46.9 11.9 %collective-permute-start.8 = (bf16[128,512]{1,0:T(8,128)(2,1)S(1)}, bf16[128,512]{1,0:T(8,128)(2,1)S(1)}, u32[]{:S(2)}, u32[]{:S(2)}) collective-permute-start(bf16[128,512]{1,0:T(8,128)(2,1)S(1)} %shard_map.100.refs_1_), channel_id=1, source_target_pairs={{0,48},{16,64},{32,80},{48,96},{64,112},{80,0},{96,16},{112,32},{1... | collective-permute-start | bytes 393224 | tf_op jit(solution)/shard_map/ppermute | solution.py:240
  50.6 8.3 %collective-permute-start.9 = (bf16[128,512]{1,0:T(8,128)(2,1)S(1)}, bf16[128,512]{1,0:T(8,128)(2,1)S(1)}, u32[]{:S(2)}, u32[]{:S(2)}) collective-permute-start(bf16[128,512]{1,0:T(8,128)(2,1)S(1)} %shard_map.100.refs_1_), channel_id=1, source_target_pairs={{0,96},{16,112},{32,0},{48,16},{64,32},{80,48},{96,64},{112,80},{1... | collective-permute-start | bytes 393224 | tf_op jit(solution)/shard_map/ppermute | solution.py:240
  58.8 4.2 %collective-permute-start.10 = (bf16[128,512]{1,0:T(8,128)(2,1)S(1)}, bf16[128,512]{1,0:T(8,128)(2,1)S(1)}, u32[]{:S(2)}, u32[]{:S(2)}) collective-permute-start(bf16[128,512]{1,0:T(8,128)(2,1)S(1)} %shard_map.101.refs_2_), channel_id=1, source_target_pairs={{0,8},{8,0},{1,9},{9,1},{2,10},{10,2},{3,11},{11,3},{4,12},{12,4},... | collective-permute-start | bytes 393224 | tf_op jit(solution)/shard_map/ppermute | solution.py:240
  58.9 8.0 %collective-permute-start.11 = (bf16[128,512]{1,0:T(8,128)(2,1)S(1)}, bf16[128,512]{1,0:T(8,128)(2,1)S(1)}, u32[]{:S(2)}, u32[]{:S(2)}) collective-permute-start(bf16[128,512]{1,0:T(8,128)(2,1)S(1)} %shard_map.101.refs_2_), channel_id=1, source_target_pairs={{0,128},{128,0},{1,129},{129,1},{2,130},{130,2},{3,131},{131,3},{4... | collective-permute-start | bytes 393224 | tf_op jit(solution)/shard_map/ppermute | solution.py:240
  61.2 7.4 %collective-permute-start.12 = (bf16[128,512]{1,0:T(8,128)(2,1)S(1)}, bf16[128,512]{1,0:T(8,128)(2,1)S(1)}, u32[]{:S(2)}, u32[]{:S(2)}) collective-permute-start(bf16[128,512]{1,0:T(8,128)(2,1)S(1)} %shard_map.101.refs_2_), channel_id=1, source_target_pairs={{0,136},{8,128},{128,8},{136,0},{1,137},{9,129},{129,9},{137,1},{2... | collective-permute-start | bytes 393224 | tf_op jit(solution)/shard_map/ppermute | solution.py:271

commit v5 on v4

--- a/solution.py
+++ b/solution.py
@@ -208,24 +208,31 @@
 
 def combine(arrived, cond, ex2, pt):
     slots = ex2.shape[0]
-    vv = arrived.shape[1]
-
-    def body(y_ref, cond_ref, ex_ref, pt_ref, out_ref, s_ref):
+    vv, hh = arrived.shape[1:]
+
+    def body(y_ref, cond_ref, ex_ref, pt_ref, out_ref, sv_ref, direct_ref):
         sv = y_ref[0].astype(F32)
         for z in range(1, Z):
             sv = sv + y_ref[z].astype(F32)
-        r = dot(sv.astype(BF), cond_ref[0])
+        for t in range(hh // 128):
+            sv_ref[t] = sv[:, t * 128 : (t + 1) * 128]
+        turned = jnp.concatenate(
+            [
+                jnp.concatenate([sv_ref[t, pl.ds(i, NV, stride=NV), :] for i in range(NV)], axis=0)
+                for t in range(hh // 128)
+            ],
+            axis=1,
+        )
+        r = dot(turned.astype(BF), cond_ref[0])
         for c in range(NC):
-            for v in range(NV):
-                block = r[v * NV : (v + 1) * NV, c * NC : (c + 1) * NC]
-                s_ref[pl.ds(v * NC + c, NV, stride=slots), :] = block
-        direct = jnp.concatenate([s_ref[v * slots : (v + 1) * slots, :] for v in range(NV)], axis=1)
-        terms = (ex_ref[...] - direct).astype(BF)
-        out_ref[...] = dot(pt_ref[...], terms).astype(BF)
-
-    return call(
-        body, pltpu.VMEM((slots, slots), BF), [], [arrived, cond, ex2, pt], (), [pltpu.VMEM((vv * NC, NC), F32)]
-    )
+            for j in range(2):
+                blocks = [r[i * NV : (i + 1) * NV, c * NC : (c + 1) * NC] for i in range(4 * j, 4 * j + 4)]
+                direct_ref[j, pl.ds(c, NV, stride=NC), :] = jnp.concatenate(blocks, axis=1)
+        direct = jnp.concatenate([direct_ref[0], direct_ref[1]], axis=1)
+        out_ref[...] = dot(pt_ref[...], (ex_ref[...] - direct).astype(BF)).astype(BF)
+
+    scratch = [pltpu.VMEM((hh // 128, vv, 128), F32), pltpu.VMEM((2, slots, 128), F32)]
+    return call(body, pltpu.VMEM((slots, slots), BF), [], [arrived, cond, ex2, pt], (), scratch)
 
 
 def finish(parts, ps):

time: 83 us -> 82.6 us (level)
  no operation moved by 1% of the time
where the time goes in v5:
time: 82.6 us; the launch traced here: 81.5 us
  waiting for transfers between devices  38.8 us (47%)
  starting transfers between devices  23.7 us (29%)
  blocking collectives  11 us (13%)
  Pallas kernels  7.19 us (9%)
    ppermute x12, waiting for transfers between devices, shift(): return lax.ppermute(x, axis, [(i, (i + by) % size) for i in range(size)])  37.1 us
    ppermute x12, starting transfers between devices, shift(): return lax.ppermute(x, axis, [(i, (i + by) % size) for i in range(size)])  14 us
    all_to_all x1, blocking collectives, per_device(): lax.all_to_all(combined.reshape(XL * Y, -1, slots), GA, 0, 0, tiled=True)  11 us
    all_to_all x1, starting transfers between devices, per_device(): arrived = lax.all_to_all(to_z, 'z', 0, 0, tiled=True)  8.6 us
    pallas_call x14, Pallas kernels, call(): pl.pallas_call(run, out_shape=out, in_specs=[SMEM] * len(scalars) + [VMEM...  7.19 us
    ppermute x1, waiting for transfers between devices, per_device(): lax.ppermute(own_half, ('xh', 'core'), [(i, 3 - i) for i in range(4)])  1.68 us
  transfers between devices with their start and end apart: 14, of which 9 were waited for; matrix products, arithmetic and copies ran while one was open for 0% of the time, Pallas kernels for 3%

profile of v5, /device:TPU:2, one launch (start us, length us, event | category | flops | bytes accessed | tf_op | source)
XLA Modules:
  0.0 81.5 jit_solution(8442438976460270977)
XLA Ops:
  0.0 1.8 %shard_map.91 = (bf16[4,64,512]{2,1,0:T(8,128)(2,1)S(1)}, bf16[32,64,128]{2,1,0:T(8,128)(2,1)S(1)}, bf16[8,512,128]{2,1,0:T(8,128)(2,1)S(1)}, s32[32]{0:T(128)S(4)}) custom-call(s32[32]{0:T(128)} %refs_0_.6, bf16[32,64,128]{2,1,0:T(8,128)(2,1)} %refs_1_.4, bf16[8,512,128]{2,1,0:T(8,128)(2,1)} %refs_2_.2), custom_call_target="tpu_custom_call" | custom-call | flops 1048576 | bytes 1048576 | tf_op jit(solution)/shard_map/pallas_call | solution.py:34
  1.8 0.1 collective-permute-start.1
  1.9 0.3 shard_map.92
  2.2 0.6 collective-permute-start
  2.7 0.6 collective-permute-done.1.refs_3_
  3.4 0.3 shard_map.93.refs_4_
  3.7 0.2 collective-permute-done.refs_3_
  3.9 0.3 shard_map.94.refs_3_
  4.2 0.5 shard_map.95
  4.7 0.5 collective-permute-start.2
  5.2 2.1 %collective-permute-start.3 = (bf16[4,64,512]{2,1,0:T(8,128)(2,1)S(1)}, bf16[4,64,512]{2,1,0:T(8,128)(2,1)S(1)}, u32[]{:S(2)}, u32[]{:S(2)}) collective-permute-start(bf16[4,64,512]{2,1,0:T(8,128)(2,1)S(1)} %shard_map.93.refs_4_), channel_id=1, source_target_pairs={{0,128},{128,0},{1,129},{129,1},{2,130},{130,2},{3,131},{131,3},{4... | collective-permute-start | bytes 786440 | tf_op jit(solution)/shard_map/ppermute | solution.py:247
  7.3 1.4 %collective-permute-start.4 = (bf16[4,64,512]{2,1,0:T(8,128)(2,1)S(1)}, bf16[4,64,512]{2,1,0:T(8,128)(2,1)S(1)}, u32[]{:S(2)}, u32[]{:S(2)}) collective-permute-start(bf16[4,64,512]{2,1,0:T(8,128)(2,1)S(1)} %shard_map.94.refs_3_), channel_id=1, source_target_pairs={{0,128},{128,0},{1,129},{129,1},{2,130},{130,2},{3,131},{131,3},{4... | collective-permute-start | bytes 786440 | tf_op jit(solution)/shard_map/ppermute | solution.py:247
  8.7 0.0 collective-permute-done.2.refs_3_
  8.7 0.5 shard_map.96.refs_0_
  9.2 6.7 %collective-permute-done.3.refs_1_ = bf16[4,64,512]{2,1,0:T(8,128)(2,1)S(1)} collective-permute-done((bf16[4,64,512]{2,1,0:T(8,128)(2,1)S(1)}, bf16[4,64,512]{2,1,0:T(8,128)(2,1)S(1)}, u32[]{:S(2)}, u32[]{:S(2)}) %collective-permute-start.3) | collective-permute-done | bytes 262176 | tf_op jit(solution)/shard_map/ppermute | solution.py:247
  15.9 4.8 %collective-permute-done.4.refs_2_ = bf16[4,64,512]{2,1,0:T(8,128)(2,1)S(1)} collective-permute-done((bf16[4,64,512]{2,1,0:T(8,128)(2,1)S(1)}, bf16[4,64,512]{2,1,0:T(8,128)(2,1)S(1)}, u32[]{:S(2)}, u32[]{:S(2)}) %collective-permute-start.4) | collective-permute-done | bytes 262176 | tf_op jit(solution)/shard_map/ppermute | solution.py:247
  20.6 0.9 %shard_map.97 = bf16[8,64,512]{2,1,0:T(8,128)(2,1)} custom-call(f32[8,64,512]{2,1,0:T(8,128)S(1)} %shard_map.96.refs_0_, bf16[4,64,512]{2,1,0:T(8,128)(2,1)S(1)} %collective-permute-done.3.refs_1_, bf16[4,64,512]{2,1,0:T(8,128)(2,1)S(1)} %collective-permute-done.4.refs_2_), custom_call_target="tpu_custom_call" | custom-call | flops 1048576 | bytes 1048576 | tf_op jit(solution)/shard_map/pallas_call | solution.py:34
  21.5 0.0 copy-start.1
  21.5 8.6 %all-to-all-start = ((bf16[8,64,512]{2,1,0:T(8,128)(2,1)}), bf16[8,64,512]{2,1,0:T(8,128)(2,1)S(1)}, u32[]{:S(2)}, u32[]{:S(2)}) async-start(bf16[8,64,512]{2,1,0:T(8,128)(2,1)} %shard_map.97), calls=%async_computation | async-start | bytes 1048576 | tf_op jit(solution)/shard_map/all_to_all | solution.py:281
  30.1 0.0 copy-done.1
  30.1 0.1 collective-permute-start.5
  30.9 0.9 %collective-permute-done.5.refs_2_ = bf16[1,256,512]{2,1,0:T(8,128)(2,1)S(1)} collective-permute-done((bf16[1,256,512]{2,1,0:T(8,128)(2,1)S(1)}, bf16[1,256,512]{2,1,0:T(8,128)(2,1)S(1)}, u32[]{:S(2)}, u32[]{:S(2)}) %collective-permute-start.5) | collective-permute-done | bytes 262176 | tf_op jit(solution)/shard_map/ppermute | solution.py:247
  31.8 2.0 %collective-permute-start.6 = (bf16[128,512]{1,0:T(8,128)(2,1)S(1)}, bf16[128,512]{1,0:T(8,128)(2,1)S(1)}, u32[]{:S(2)}, u32[]{:S(2)}) collective-permute-start(bf16[128,512]{1,0:T(8,128)(2,1)S(1)} %shard_map.99.refs_1_), channel_id=1, source_target_pairs={{0,16},{16,32},{32,48},{48,64},{64,80},{80,96},{96,112},{112,0},{1... | collective-permute-start | bytes 393224 | tf_op jit(solution)/shard_map/ppermute | solution.py:247
  33.8 1.3 %collective-permute-start.7 = (bf16[128,512]{1,0:T(8,128)(2,1)S(1)}, bf16[128,512]{1,0:T(8,128)(2,1)S(1)}, u32[]{:S(2)}, u32[]{:S(2)}) collective-permute-start(bf16[128,512]{1,0:T(8,128)(2,1)S(1)} %shard_map.99.refs_1_), channel_id=1, source_target_pairs={{0,112},{16,0},{32,16},{48,32},{64,48},{80,64},{96,80},{112,96},{1... | collective-permute-start | bytes 393224 | tf_op jit(solution)/shard_map/ppermute | solution.py:247
  35.1 11.8 %collective-permute-done.6.refs_2_ = bf16[128,512]{1,0:T(8,128)(2,1)S(1)} collective-permute-done((bf16[128,512]{1,0:T(8,128)(2,1)S(1)}, bf16[128,512]{1,0:T(8,128)(2,1)S(1)}, u32[]{:S(2)}, u32[]{:S(2)}) %collective-permute-start.6) | collective-permute-done | bytes 131104 | tf_op jit(solution)/shard_map/ppermute | solution.py:247
  46.9 0.0 collective-permute-done.7.refs_3_
  46.9 0.0 copy-start.4
  46.9 0.0 copy-start
  46.9 3.6 %collective-permute-start.8 = (bf16[128,512]{1,0:T(8,128)(2,1)S(1)}, bf16[128,512]{1,0:T(8,128)(2,1)S(1)}, u32[]{:S(2)}, u32[]{:S(2)}) collective-permute-start(bf16[128,512]{1,0:T(8,128)(2,1)S(1)} %shard_map.100.refs_1_), channel_id=1, source_target_pairs={{0,48},{16,64},{32,80},{48,96},{64,112},{80,0},{96,16},{112,32},{1... | collective-permute-start | bytes 393224 | tf_op jit(solution)/shard_map/ppermute | solution.py:247
  50.6 0.0 collective-permute-start.9
  50.6 8.3 %collective-permute-done.8.refs_2_ = bf16[128,512]{1,0:T(8,128)(2,1)S(1)} collective-permute-done((bf16[128,512]{1,0:T(8,128)(2,1)S(1)}, bf16[128,512]{1,0:T(8,128)(2,1)S(1)}, u32[]{:S(2)}, u32[]{:S(2)}) %collective-permute-start.8) | collective-permute-done | bytes 131104 | tf_op jit(solution)/shard_map/ppermute | solution.py:247
  58.8 0.0 collective-permute-done.9.refs_3_
  58.8 0.1 collective-permute-start.10
  58.9 2.2 %collective-permute-start.11 = (bf16[128,512]{1,0:T(8,128)(2,1)S(1)}, bf16[128,512]{1,0:T(8,128)(2,1)S(1)}, u32[]{:S(2)}, u32[]{:S(2)}) collective-permute-start(bf16[128,512]{1,0:T(8,128)(2,1)S(1)} %shard_map.101.refs_2_), channel_id=1, source_target_pairs={{0,128},{128,0},{1,129},{129,1},{2,130},{130,2},{3,131},{131,3},{4... | collective-permute-start | bytes 393224 | tf_op jit(solution)/shard_map/ppermute | solution.py:247
  61.2 1.1 %collective-permute-start.12 = (bf16[128,512]{1,0:T(8,128)(2,1)S(1)}, bf16[128,512]{1,0:T(8,128)(2,1)S(1)}, u32[]{:S(2)}, u32[]{:S(2)}) collective-permute-start(bf16[128,512]{1,0:T(8,128)(2,1)S(1)} %shard_map.101.refs_2_), channel_id=1, source_target_pairs={{0,136},{8,128},{128,8},{136,0},{1,137},{9,129},{129,9},{137,1},{2... | collective-permute-start | bytes 393224 | tf_op jit(solution)/shard_map/ppermute | solution.py:278
  62.3 0.0 copy-done.4
  62.3 0.0 copy-done.2
  62.3 0.0 copy-done.3
  62.3 0.7 shard_map.98
  63.0 0.0 collective-permute-done.10.refs_3_
  63.0 3.9 %collective-permute-done.11.refs_4_ = bf16[128,512]{1,0:T(8,128)(2,1)S(1)} collective-permute-done((bf16[128,512]{1,0:T(8,128)(2,1)S(1)}, bf16[128,512]{1,0:T(8,128)(2,1)S(1)}, u32[]{:S(2)}, u32[]{:S(2)}) %collective-permute-start.11) | collective-permute-done | bytes 131104 | tf_op jit(solution)/shard_map/ppermute | solution.py:247
  66.9 1.7 %collective-permute-done.12.refs_5_ = bf16[128,512]{1,0:T(8,128)(2,1)S(1)} collective-permute-done((bf16[128,512]{1,0:T(8,128)(2,1)S(1)}, bf16[128,512]{1,0:T(8,128)(2,1)S(1)}, u32[]{:S(2)}, u32[]{:S(2)}) %collective-permute-start.12) | collective-permute-done | bytes 131104 | tf_op jit(solution)/shard_map/ppermute | solution.py:278
  68.6 0.3 shard_map.102.refs_2_
  68.9 0.0 all-to-all-done.refs_0_
  68.9 0.0 copy-done
  68.9 0.9 %shard_map.103 = bf16[256,256]{1,0:T(8,128)(2,1)S(1)} custom-call(bf16[8,64,512]{2,1,0:T(8,128)(2,1)S(1)} %all-to-all-done.refs_0_, bf16[1,1024,512]{2,1,0:T(8,128)(2,1)S(1)} %copy-done, f32[256,256]{1,0:T(8,128)S(1)} %shard_map.102.refs_2_, bf16[256,256]{1,0:T(8,128)(2,1)S(1)} %get-tuple-element.17.refs_3_), custom_call_target="tpu_custom_call" | custom-call | flops 1048576 | bytes 1048576 | tf_op jit(solution)/shard_map/pallas_call | solution.py:34
  69.8 11.0 %all_to_all.10.refs_0_ = bf16[8,32,256]{2,1,0:T(8,128)(2,1)S(1)} all-to-all(bf16[8,32,256]{2,1,0:T(8,128)(2,1)S(1)} %bitcast.2), channel_id=1, replica_groups=mesh['xh'=2,'z'=8,'core'=2,'xl'=2,'y'=4] {'xl','y'}, dimensions={0} | all-to-all | bytes 262144 | tf_op jit(solution)/shard_map/all_to_all | solution.py:285
  80.7 0.8 shard_map.104
  (6 shorter events, 0.1 us)
Async XLA Ops:
  1.8 1.6 %collective-permute-start.1 = (bf16[4,64,512]{2,1,0:T(8,128)(2,1)S(1)}, bf16[4,64,512]{2,1,0:T(8,128)(2,1)S(1)}, u32[]{:S(2)}, u32[]{:S(2)}) collective-permute-start(bf16[4,64,512]{2,1,0:T(8,128)(2,1)S(1)} %get-tuple-element.15), channel_id=1, source_target_pairs={{0,8},{8,0},{1,9},{9,1},{2,10},{10,2},{3,11},{11,3},{4,12},{12,4},... | collective-permute-start | bytes 786440 | tf_op jit(solution)/shard_map/ppermute | solution.py:247
  2.2 1.7 %collective-permute-start = (bf16[4,64,512]{2,1,0:T(8,128)(2,1)S(1)}, bf16[4,64,512]{2,1,0:T(8,128)(2,1)S(1)}, u32[]{:S(2)}, u32[]{:S(2)}) collective-permute-start(bf16[4,64,512]{2,1,0:T(8,128)(2,1)S(1)} %shard_map.92), channel_id=1, source_target_pairs={{0,8},{8,0},{1,9},{9,1},{2,10},{10,2},{3,11},{11,3},{4,12},{12,4},... | collective-permute-start | bytes 786440 | tf_op jit(solution)/shard_map/ppermute | solution.py:247
  4.7 4.0 %collective-permute-start.2 = (bf16[8,64,512]{2,1,0:T(8,128)(2,1)S(1)}, bf16[8,64,512]{2,1,0:T(8,128)(2,1)S(1)}, u32[]{:S(2)}, u32[]{:S(2)}) collective-permute-start(bf16[8,64,512]{2,1,0:T(8,128)(2,1)S(1)} %shard_map.95), channel_id=1, source_target_pairs={{0,8},{8,0},{1,9},{9,1},{2,10},{10,2},{3,11},{11,3},{4,12},{12,4},... | collective-permute-start | bytes 1572872 | tf_op jit(solution)/shard_map/ppermute | solution.py:247
  5.2 10.7 %collective-permute-start.3 = (bf16[4,64,512]{2,1,0:T(8,128)(2,1)S(1)}, bf16[4,64,512]{2,1,0:T(8,128)(2,1)S(1)}, u32[]{:S(2)}, u32[]{:S(2)}) collective-permute-start(bf16[4,64,512]{2,1,0:T(8,128)(2,1)S(1)} %shard_map.93.refs_4_), channel_id=1, source_target_pairs={{0,128},{128,0},{1,129},{129,1},{2,130},{130,2},{3,131},{131,3},{4... | collective-permute-start | bytes 786440 | tf_op jit(solution)/shard_map/ppermute | solution.py:247
  7.3 13.3 %collective-permute-start.4 = (bf16[4,64,512]{2,1,0:T(8,128)(2,1)S(1)}, bf16[4,64,512]{2,1,0:T(8,128)(2,1)S(1)}, u32[]{:S(2)}, u32[]{:S(2)}) collective-permute-start(bf16[4,64,512]{2,1,0:T(8,128)(2,1)S(1)} %shard_map.94.refs_3_), channel_id=1, source_target_pairs={{0,128},{128,0},{1,129},{129,1},{2,130},{130,2},{3,131},{131,3},{4... | collective-permute-start | bytes 786440 | tf_op jit(solution)/shard_map/ppermute | solution.py:247
  21.5 8.6 %copy-start.1 = (bf16[1,256,512]{2,1,0:T(8,128)(2,1)S(1)}, bf16[1,256,512]{2,1,0:T(8,128)(2,1)}, u32[]{:S(2)}) copy-start(bf16[1,256,512]{2,1,0:T(8,128)(2,1)} %refs_1_.6) | copy-start | bytes 786436
  21.5 47.3 %all-to-all-start = ((bf16[8,64,512]{2,1,0:T(8,128)(2,1)}), bf16[8,64,512]{2,1,0:T(8,128)(2,1)S(1)}, u32[]{:S(2)}, u32[]{:S(2)}) async-start(bf16[8,64,512]{2,1,0:T(8,128)(2,1)} %shard_map.97), calls=%async_computation | async-start | bytes 1048576 | tf_op jit(solution)/shard_map/all_to_all | solution.py:281
  30.1 1.6 %collective-permute-start.5 = (bf16[1,256,512]{2,1,0:T(8,128)(2,1)S(1)}, bf16[1,256,512]{2,1,0:T(8,128)(2,1)S(1)}, u32[]{:S(2)}, u32[]{:S(2)}) collective-permute-start(bf16[1,256,512]{2,1,0:T(8,128)(2,1)S(1)} %copy-done.1), channel_id=1, source_target_pairs={{0,8},{8,0},{1,9},{9,1},{2,10},{10,2},{3,11},{11,3},{4,12},{12,4},... | collective-permute-start | bytes 786440 | tf_op jit(solution)/shard_map/ppermute | solution.py:247
  31.8 15.1 %collective-permute-start.6 = (bf16[128,512]{1,0:T(8,128)(2,1)S(1)}, bf16[128,512]{1,0:T(8,128)(2,1)S(1)}, u32[]{:S(2)}, u32[]{:S(2)}) collective-permute-start(bf16[128,512]{1,0:T(8,128)(2,1)S(1)} %shard_map.99.refs_1_), channel_id=1, source_target_pairs={{0,16},{16,32},{32,48},{48,64},{64,80},{80,96},{96,112},{112,0},{1... | collective-permute-start | bytes 393224 | tf_op jit(solution)/shard_map/ppermute | solution.py:247
  33.8 13.1 %collective-permute-start.7 = (bf16[128,512]{1,0:T(8,128)(2,1)S(1)}, bf16[128,512]{1,0:T(8,128)(2,1)S(1)}, u32[]{:S(2)}, u32[]{:S(2)}) collective-permute-start(bf16[128,512]{1,0:T(8,128)(2,1)S(1)} %shard_map.99.refs_1_), channel_id=1, source_target_pairs={{0,112},{16,0},{32,16},{48,32},{64,48},{80,64},{96,80},{112,96},{1... | collective-permute-start | bytes 393224 | tf_op jit(solution)/shard_map/ppermute | solution.py:247
  46.9 15.4 %copy-start.4 = (bf16[512]{0:T(512)(128)(2,1)S(1)}, bf16[512]{0:T(512)(128)(2,1)}, u32[]{:S(2)}) copy-start(bf16[512]{0:T(512)(128)(2,1)} %param.13) | copy-start | bytes 3076
  46.9 15.4 %copy-start.2 = (s32[32,256]{1,0:T(8,128)S(1)}, s32[32,256]{1,0:T(8,128)}, u32[]{:S(2)}) copy-start(s32[32,256]{1,0:T(8,128)} %refs_2_.3) | copy-start | bytes 98308
  46.9 15.4 %copy-start.3 = (s32[32]{0:T(128)S(1)}, s32[32]{0:T(128)}, u32[]{:S(2)}) copy-start(s32[32]{0:T(128)} %refs_1_.5) | copy-start | bytes 388
  46.9 22.0 %copy-start = (bf16[1,1024,512]{2,1,0:T(8,128)(2,1)S(1)}, bf16[1,1024,512]{2,1,0:T(8,128)(2,1)}, u32[]{:S(2)}) copy-start(bf16[1,1024,512]{2,1,0:T(8,128)(2,1)} %refs_1_.7) | copy-start | bytes 3145732
  46.9 11.9 %collective-permute-start.8 = (bf16[128,512]{1,0:T(8,128)(2,1)S(1)}, bf16[128,512]{1,0:T(8,128)(2,1)S(1)}, u32[]{:S(2)}, u32[]{:S(2)}) collective-permute-start(bf16[128,512]{1,0:T(8,128)(2,1)S(1)} %shard_map.100.refs_1_), channel_id=1, source_target_pairs={{0,48},{16,64},{32,80},{48,96},{64,112},{80,0},{96,16},{112,32},{1... | collective-permute-start | bytes 393224 | tf_op jit(solution)/shard_map/ppermute | solution.py:247
  50.6 8.3 %collective-permute-start.9 = (bf16[128,512]{1,0:T(8,128)(2,1)S(1)}, bf16[128,512]{1,0:T(8,128)(2,1)S(1)}, u32[]{:S(2)}, u32[]{:S(2)}) collective-permute-start(bf16[128,512]{1,0:T(8,128)(2,1)S(1)} %shard_map.100.refs_1_), channel_id=1, source_target_pairs={{0,96},{16,112},{32,0},{48,16},{64,32},{80,48},{96,64},{112,80},{1... | collective-permute-start | bytes 393224 | tf_op jit(solution)/shard_map/ppermute | solution.py:247
  58.8 4.2 %collective-permute-start.10 = (bf16[128,512]{1,0:T(8,128)(2,1)S(1)}, bf16[128,512]{1,0:T(8,128)(2,1)S(1)}, u32[]{:S(2)}, u32[]{:S(2)}) collective-permute-start(bf16[128,512]{1,0:T(8,128)(2,1)S(1)} %shard_map.101.refs_2_), channel_id=1, source_target_pairs={{0,8},{8,0},{1,9},{9,1},{2,10},{10,2},{3,11},{11,3},{4,12},{12,4},... | collective-permute-start | bytes 393224 | tf_op jit(solution)/shard_map/ppermute | solution.py:247
  58.9 8.0 %collective-permute-start.11 = (bf16[128,512]{1,0:T(8,128)(2,1)S(1)}, bf16[128,512]{1,0:T(8,128)(2,1)S(1)}, u32[]{:S(2)}, u32[]{:S(2)}) collective-permute-start(bf16[128,512]{1,0:T(8,128)(2,1)S(1)} %shard_map.101.refs_2_), channel_id=1, source_target_pairs={{0,128},{128,0},{1,129},{129,1},{2,130},{130,2},{3,131},{131,3},{4... | collective-permute-start | bytes 393224 | tf_op jit(solution)/shard_map/ppermute | solution.py:247
  61.2 7.4 %collective-permute-start.12 = (bf16[128,512]{1,0:T(8,128)(2,1)S(1)}, bf16[128,512]{1,0:T(8,128)(2,1)S(1)}, u32[]{:S(2)}, u32[]{:S(2)}) collective-permute-start(bf16[128,512]{1,0:T(8,128)(2,1)S(1)} %shard_map.101.refs_2_), channel_id=1, source_target_pairs={{0,136},{8,128},{128,8},{136,0},{1,137},{9,129},{129,9},{137,1},{2... | collective-permute-start | bytes 393224 | tf_op jit(solution)/shard_map/ppermute | solution.py:278

commit v6 on v5

--- a/solution.py
+++ b/solution.py
@@ -168,15 +168,24 @@
     return call(body, pltpu.VMEM(own.shape, BF), [column], [own, below, above])
 
 
-def add(own, low, high):
-    half = low.shape[0]
-
-    def body(own_ref, low_ref, high_ref, out_ref):
-        for z in range(Z):
-            arrived = (low_ref if z < half else high_ref)[z % half]
-            out_ref[z] = (own_ref[z] + arrived.astype(F32)).astype(BF)
-
-    return call(body, pltpu.VMEM(own.shape, BF), [], [own, low, high])
+def add(own, arrived, part, begun=None):
+    half = arrived.shape[0]
+
+    def body(own_ref, in_ref, *refs):
+        for z in range(half):
+            refs[-1][z] = (own_ref[part * half + z] + in_ref[z].astype(F32)).astype(BF)
+
+    more = () if begun is None else (begun,)
+    return pl.pallas_call(
+        body,
+        out_shape=jax.ShapeDtypeStruct(own.shape, BF),
+        in_specs=[VMEM, VMEM] + [ANY for _ in more],
+        grid=(1,),
+        out_specs=pl.BlockSpec((half,) + own.shape[1:], lambda i: (part, 0, 0)),
+        input_output_aliases={2: 0} if more else {},
+        compiler_params=pltpu.CompilerParams(vmem_limit_bytes=12 << 20),
+        cost_estimate=pl.CostEstimate(flops=1 << 20, bytes_accessed=1 << 19, transcendentals=0),
+    )(own, arrived, *more)
 
 
 def exchange_terms(column, weighted, halves):
@@ -277,7 +286,8 @@
     own_x = swap(own_half, "xh")
     sib_x = lax.ppermute(own_half, ("xh", "core"), [(i, 3 - i) for i in range(4)])
     sib_half = swap(own_half, "core")
-    to_z = add(own, near(low), near(high))
+    begun = add(own, near(low), 0)
+    to_z = add(own, near(high), 1, begun)
     arrived = lax.all_to_all(to_z, "z", 0, 0, tiled=True)
     halves = [near(a) for a in (own_half, sib_half, own_x, sib_x)]
     ex2 = exchange_terms(column_k, weighted, halves)

time: 82.6 us -> 82.4 us (level)
    pallas_call x0 -> x2, Pallas kernels: none -> 1.48 us  [add(): pl.pallas_call(body, out_shape=jax.ShapeDtypeStruct(own.shape, BF), in_sp...]
    pallas_call x14 -> x13, Pallas kernels: 7.19 us -> 6.3 us  [call(): pl.pallas_call(run, out_shape=out, in_specs=[SMEM] * len(scalars) + [VMEM...]
  transfers between devices with their start and end apart: 14 -> 14, of which waited for: 9 -> 9; matrix products, arithmetic and copies ran while one was open for 0% -> 0% of each run, Pallas kernels for 3% -> 4%
where the time goes in v6:
time: 82.4 us; the launch traced here: 81.3 us
  waiting for transfers between devices  38 us (46%)
  starting transfers between devices  23.7 us (29%)
  blocking collectives  11 us (13%)
  Pallas kernels  7.78 us (9%)
    ppermute x12, waiting for transfers between devices, shift(): return lax.ppermute(x, axis, [(i, (i + by) % size) for i in range(size)])  36.4 us
    ppermute x12, starting transfers between devices, shift(): return lax.ppermute(x, axis, [(i, (i + by) % size) for i in range(size)])  14 us
    all_to_all x1, blocking collectives, per_device(): lax.all_to_all(combined.reshape(XL * Y, -1, slots), GA, 0, 0, tiled=True)  11 us
    all_to_all x1, starting transfers between devices, per_device(): arrived = lax.all_to_all(to_z, 'z', 0, 0, tiled=True)  8.6 us
    pallas_call x13, Pallas kernels, call(): pl.pallas_call(run, out_shape=out, in_specs=[SMEM] * len(scalars) + [VMEM...  6.3 us
    ppermute x1, waiting for transfers between devices, per_device(): lax.ppermute(own_half, ('xh', 'core'), [(i, 3 - i) for i in range(4)])  1.68 us
  transfers between devices with their start and end apart: 14, of which 9 were waited for; matrix products, arithmetic and copies ran while one was open for 0% of the time, Pallas kernels for 4%

profile of v6, /device:TPU:2, one launch (start us, length us, event | category | flops | bytes accessed | tf_op | source)
XLA Modules:
  0.0 81.3 jit_solution(8891982070203559114)
XLA Ops:
  0.0 1.8 %shard_map.91 = (bf16[4,64,512]{2,1,0:T(8,128)(2,1)S(1)}, bf16[32,64,128]{2,1,0:T(8,128)(2,1)S(1)}, bf16[8,512,128]{2,1,0:T(8,128)(2,1)S(1)}, s32[32]{0:T(128)S(4)}) custom-call(s32[32]{0:T(128)} %refs_0_.6, bf16[32,64,128]{2,1,0:T(8,128)(2,1)} %refs_1_.4, bf16[8,512,128]{2,1,0:T(8,128)(2,1)} %refs_2_.2), custom_call_target="tpu_custom_call" | custom-call | flops 1048576 | bytes 1048576 | tf_op jit(solution)/shard_map/pallas_call | solution.py:34
  1.8 0.1 collective-permute-start.1
  1.9 0.3 shard_map.92
  2.2 0.6 collective-permute-start
  2.7 0.6 collective-permute-done.1.refs_3_
  3.4 0.3 shard_map.93.refs_4_
  3.7 0.2 collective-permute-done.refs_3_
  3.9 0.3 shard_map.94.refs_3_
  4.2 0.5 shard_map.95
  4.7 0.5 collective-permute-start.2
  5.2 2.1 %collective-permute-start.4 = (bf16[4,64,512]{2,1,0:T(8,128)(2,1)S(1)}, bf16[4,64,512]{2,1,0:T(8,128)(2,1)S(1)}, u32[]{:S(2)}, u32[]{:S(2)}) collective-permute-start(bf16[4,64,512]{2,1,0:T(8,128)(2,1)S(1)} %shard_map.93.refs_4_), channel_id=1, source_target_pairs={{0,128},{128,0},{1,129},{129,1},{2,130},{130,2},{3,131},{131,3},{4... | collective-permute-start | bytes 786440 | tf_op jit(solution)/shard_map/ppermute | solution.py:256
  7.3 1.4 %collective-permute-start.3 = (bf16[4,64,512]{2,1,0:T(8,128)(2,1)S(1)}, bf16[4,64,512]{2,1,0:T(8,128)(2,1)S(1)}, u32[]{:S(2)}, u32[]{:S(2)}) collective-permute-start(bf16[4,64,512]{2,1,0:T(8,128)(2,1)S(1)} %shard_map.94.refs_3_), channel_id=1, source_target_pairs={{0,128},{128,0},{1,129},{129,1},{2,130},{130,2},{3,131},{131,3},{4... | collective-permute-start | bytes 786440 | tf_op jit(solution)/shard_map/ppermute | solution.py:256
  8.7 0.0 collective-permute-done.2.refs_3_
  8.7 0.5 shard_map.96.own_ref
  9.2 6.7 %collective-permute-done.4.in_ref = bf16[4,64,512]{2,1,0:T(8,128)(2,1)S(1)} collective-permute-done((bf16[4,64,512]{2,1,0:T(8,128)(2,1)S(1)}, bf16[4,64,512]{2,1,0:T(8,128)(2,1)S(1)}, u32[]{:S(2)}, u32[]{:S(2)}) %collective-permute-start.4) | collective-permute-done | bytes 262176 | tf_op jit(solution)/shard_map/ppermute | solution.py:256
  15.9 0.7 shard_map.97.refs_0_
  16.6 4.0 %collective-permute-done.3.in_ref = bf16[4,64,512]{2,1,0:T(8,128)(2,1)S(1)} collective-permute-done((bf16[4,64,512]{2,1,0:T(8,128)(2,1)S(1)}, bf16[4,64,512]{2,1,0:T(8,128)(2,1)S(1)}, u32[]{:S(2)}, u32[]{:S(2)}) %collective-permute-start.3) | collective-permute-done | bytes 262176 | tf_op jit(solution)/shard_map/ppermute | solution.py:256
  20.6 0.7 shard_map.98
  21.4 0.0 copy-start.1
  21.4 8.6 %all-to-all-start = ((bf16[8,64,512]{2,1,0:T(8,128)(2,1)}), bf16[8,64,512]{2,1,0:T(8,128)(2,1)S(1)}, u32[]{:S(2)}, u32[]{:S(2)}) async-start(bf16[8,64,512]{2,1,0:T(8,128)(2,1)} %shard_map.98), calls=%async_computation | async-start | bytes 1048576 | tf_op jit(solution)/shard_map/all_to_all | solution.py:291
  30.0 0.0 copy-done.1
  30.0 0.1 collective-permute-start.5
  30.7 0.9 %collective-permute-done.5.refs_2_ = bf16[1,256,512]{2,1,0:T(8,128)(2,1)S(1)} collective-permute-done((bf16[1,256,512]{2,1,0:T(8,128)(2,1)S(1)}, bf16[1,256,512]{2,1,0:T(8,128)(2,1)S(1)}, u32[]{:S(2)}, u32[]{:S(2)}) %collective-permute-start.5) | collective-permute-done | bytes 262176 | tf_op jit(solution)/shard_map/ppermute | solution.py:256
  31.6 2.0 %collective-permute-start.6 = (bf16[128,512]{1,0:T(8,128)(2,1)S(1)}, bf16[128,512]{1,0:T(8,128)(2,1)S(1)}, u32[]{:S(2)}, u32[]{:S(2)}) collective-permute-start(bf16[128,512]{1,0:T(8,128)(2,1)S(1)} %shard_map.100.refs_1_), channel_id=1, source_target_pairs={{0,16},{16,32},{32,48},{48,64},{64,80},{80,96},{96,112},{112,0},{1... | collective-permute-start | bytes 393224 | tf_op jit(solution)/shard_map/ppermute | solution.py:256
  33.6 1.3 %collective-permute-start.7 = (bf16[128,512]{1,0:T(8,128)(2,1)S(1)}, bf16[128,512]{1,0:T(8,128)(2,1)S(1)}, u32[]{:S(2)}, u32[]{:S(2)}) collective-permute-start(bf16[128,512]{1,0:T(8,128)(2,1)S(1)} %shard_map.100.refs_1_), channel_id=1, source_target_pairs={{0,112},{16,0},{32,16},{48,32},{64,48},{80,64},{96,80},{112,96},{1... | collective-permute-start | bytes 393224 | tf_op jit(solution)/shard_map/ppermute | solution.py:256
  34.9 11.8 %collective-permute-done.6.refs_2_ = bf16[128,512]{1,0:T(8,128)(2,1)S(1)} collective-permute-done((bf16[128,512]{1,0:T(8,128)(2,1)S(1)}, bf16[128,512]{1,0:T(8,128)(2,1)S(1)}, u32[]{:S(2)}, u32[]{:S(2)}) %collective-permute-start.6) | collective-permute-done | bytes 131104 | tf_op jit(solution)/shard_map/ppermute | solution.py:256
  46.7 0.0 collective-permute-done.7.refs_3_
  46.8 0.0 copy-start
  46.8 3.6 %collective-permute-start.8 = (bf16[128,512]{1,0:T(8,128)(2,1)S(1)}, bf16[128,512]{1,0:T(8,128)(2,1)S(1)}, u32[]{:S(2)}, u32[]{:S(2)}) collective-permute-start(bf16[128,512]{1,0:T(8,128)(2,1)S(1)} %shard_map.101.refs_1_), channel_id=1, source_target_pairs={{0,48},{16,64},{32,80},{48,96},{64,112},{80,0},{96,16},{112,32},{1... | collective-permute-start | bytes 393224 | tf_op jit(solution)/shard_map/ppermute | solution.py:256
  50.4 0.0 collective-permute-start.9
  50.4 8.3 %collective-permute-done.8.refs_2_ = bf16[128,512]{1,0:T(8,128)(2,1)S(1)} collective-permute-done((bf16[128,512]{1,0:T(8,128)(2,1)S(1)}, bf16[128,512]{1,0:T(8,128)(2,1)S(1)}, u32[]{:S(2)}, u32[]{:S(2)}) %collective-permute-start.8) | collective-permute-done | bytes 131104 | tf_op jit(solution)/shard_map/ppermute | solution.py:256
  58.7 0.0 collective-permute-done.9.refs_3_
  58.7 0.1 collective-permute-start.10
  58.8 2.2 %collective-permute-start.11 = (bf16[128,512]{1,0:T(8,128)(2,1)S(1)}, bf16[128,512]{1,0:T(8,128)(2,1)S(1)}, u32[]{:S(2)}, u32[]{:S(2)}) collective-permute-start(bf16[128,512]{1,0:T(8,128)(2,1)S(1)} %shard_map.102.refs_2_), channel_id=1, source_target_pairs={{0,128},{128,0},{1,129},{129,1},{2,130},{130,2},{3,131},{131,3},{4... | collective-permute-start | bytes 393224 | tf_op jit(solution)/shard_map/ppermute | solution.py:256
  61.0 1.1 %collective-permute-start.12 = (bf16[128,512]{1,0:T(8,128)(2,1)S(1)}, bf16[128,512]{1,0:T(8,128)(2,1)S(1)}, u32[]{:S(2)}, u32[]{:S(2)}) collective-permute-start(bf16[128,512]{1,0:T(8,128)(2,1)S(1)} %shard_map.102.refs_2_), channel_id=1, source_target_pairs={{0,136},{8,128},{128,8},{136,0},{1,137},{9,129},{129,9},{137,1},{2... | collective-permute-start | bytes 393224 | tf_op jit(solution)/shard_map/ppermute | solution.py:287
  62.1 0.0 copy-done.4
  62.1 0.0 copy-done.2
  62.1 0.0 copy-done.3
  62.2 0.7 shard_map.99
  62.8 0.0 collective-permute-done.10.refs_3_
  62.8 3.9 %collective-permute-done.11.refs_4_ = bf16[128,512]{1,0:T(8,128)(2,1)S(1)} collective-permute-done((bf16[128,512]{1,0:T(8,128)(2,1)S(1)}, bf16[128,512]{1,0:T(8,128)(2,1)S(1)}, u32[]{:S(2)}, u32[]{:S(2)}) %collective-permute-start.11) | collective-permute-done | bytes 131104 | tf_op jit(solution)/shard_map/ppermute | solution.py:256
  66.7 1.7 %collective-permute-done.12.refs_5_ = bf16[128,512]{1,0:T(8,128)(2,1)S(1)} collective-permute-done((bf16[128,512]{1,0:T(8,128)(2,1)S(1)}, bf16[128,512]{1,0:T(8,128)(2,1)S(1)}, u32[]{:S(2)}, u32[]{:S(2)}) %collective-permute-start.12) | collective-permute-done | bytes 131104 | tf_op jit(solution)/shard_map/ppermute | solution.py:287
  68.4 0.3 shard_map.103.refs_2_
  68.7 0.0 all-to-all-done.refs_0_
  68.7 0.0 copy-done
  68.7 0.9 %shard_map.104 = bf16[256,256]{1,0:T(8,128)(2,1)S(1)} custom-call(bf16[8,64,512]{2,1,0:T(8,128)(2,1)S(1)} %all-to-all-done.refs_0_, bf16[1,1024,512]{2,1,0:T(8,128)(2,1)S(1)} %copy-done, f32[256,256]{1,0:T(8,128)S(1)} %shard_map.103.refs_2_, bf16[256,256]{1,0:T(8,128)(2,1)S(1)} %get-tuple-element.17.refs_3_), custom_call_target="tpu_custom_call" | custom-call | flops 1048576 | bytes 1048576 | tf_op jit(solution)/shard_map/pallas_call | solution.py:34
  69.6 11.0 %all_to_all.10.refs_0_ = bf16[8,32,256]{2,1,0:T(8,128)(2,1)S(1)} all-to-all(bf16[8,32,256]{2,1,0:T(8,128)(2,1)S(1)} %bitcast.2), channel_id=1, replica_groups=mesh['xh'=2,'z'=8,'core'=2,'xl'=2,'y'=4] {'xl','y'}, dimensions={0} | all-to-all | bytes 262144 | tf_op jit(solution)/shard_map/all_to_all | solution.py:295
  80.6 0.8 shard_map.105
  (7 shorter events, 0.1 us)
Async XLA Ops:
  1.8 1.6 %collective-permute-start.1 = (bf16[4,64,512]{2,1,0:T(8,128)(2,1)S(1)}, bf16[4,64,512]{2,1,0:T(8,128)(2,1)S(1)}, u32[]{:S(2)}, u32[]{:S(2)}) collective-permute-start(bf16[4,64,512]{2,1,0:T(8,128)(2,1)S(1)} %get-tuple-element.15), channel_id=1, source_target_pairs={{0,8},{8,0},{1,9},{9,1},{2,10},{10,2},{3,11},{11,3},{4,12},{12,4},... | collective-permute-start | bytes 786440 | tf_op jit(solution)/shard_map/ppermute | solution.py:256
  2.2 1.7 %collective-permute-start = (bf16[4,64,512]{2,1,0:T(8,128)(2,1)S(1)}, bf16[4,64,512]{2,1,0:T(8,128)(2,1)S(1)}, u32[]{:S(2)}, u32[]{:S(2)}) collective-permute-start(bf16[4,64,512]{2,1,0:T(8,128)(2,1)S(1)} %shard_map.92), channel_id=1, source_target_pairs={{0,8},{8,0},{1,9},{9,1},{2,10},{10,2},{3,11},{11,3},{4,12},{12,4},... | collective-permute-start | bytes 786440 | tf_op jit(solution)/shard_map/ppermute | solution.py:256
  4.7 4.0 %collective-permute-start.2 = (bf16[8,64,512]{2,1,0:T(8,128)(2,1)S(1)}, bf16[8,64,512]{2,1,0:T(8,128)(2,1)S(1)}, u32[]{:S(2)}, u32[]{:S(2)}) collective-permute-start(bf16[8,64,512]{2,1,0:T(8,128)(2,1)S(1)} %shard_map.95), channel_id=1, source_target_pairs={{0,8},{8,0},{1,9},{9,1},{2,10},{10,2},{3,11},{11,3},{4,12},{12,4},... | collective-permute-start | bytes 1572872 | tf_op jit(solution)/shard_map/ppermute | solution.py:256
  5.2 10.7 %collective-permute-start.4 = (bf16[4,64,512]{2,1,0:T(8,128)(2,1)S(1)}, bf16[4,64,512]{2,1,0:T(8,128)(2,1)S(1)}, u32[]{:S(2)}, u32[]{:S(2)}) collective-permute-start(bf16[4,64,512]{2,1,0:T(8,128)(2,1)S(1)} %shard_map.93.refs_4_), channel_id=1, source_target_pairs={{0,128},{128,0},{1,129},{129,1},{2,130},{130,2},{3,131},{131,3},{4... | collective-permute-start | bytes 786440 | tf_op jit(solution)/shard_map/ppermute | solution.py:256
  7.3 13.3 %collective-permute-start.3 = (bf16[4,64,512]{2,1,0:T(8,128)(2,1)S(1)}, bf16[4,64,512]{2,1,0:T(8,128)(2,1)S(1)}, u32[]{:S(2)}, u32[]{:S(2)}) collective-permute-start(bf16[4,64,512]{2,1,0:T(8,128)(2,1)S(1)} %shard_map.94.refs_3_), channel_id=1, source_target_pairs={{0,128},{128,0},{1,129},{129,1},{2,130},{130,2},{3,131},{131,3},{4... | collective-permute-start | bytes 786440 | tf_op jit(solution)/shard_map/ppermute | solution.py:256
  21.4 8.6 %copy-start.1 = (bf16[1,256,512]{2,1,0:T(8,128)(2,1)S(1)}, bf16[1,256,512]{2,1,0:T(8,128)(2,1)}, u32[]{:S(2)}) copy-start(bf16[1,256,512]{2,1,0:T(8,128)(2,1)} %refs_1_.6) | copy-start | bytes 786436
  21.4 47.3 %all-to-all-start = ((bf16[8,64,512]{2,1,0:T(8,128)(2,1)}), bf16[8,64,512]{2,1,0:T(8,128)(2,1)S(1)}, u32[]{:S(2)}, u32[]{:S(2)}) async-start(bf16[8,64,512]{2,1,0:T(8,128)(2,1)} %shard_map.98), calls=%async_computation | async-start | bytes 1048576 | tf_op jit(solution)/shard_map/all_to_all | solution.py:291
  30.0 1.6 %collective-permute-start.5 = (bf16[1,256,512]{2,1,0:T(8,128)(2,1)S(1)}, bf16[1,256,512]{2,1,0:T(8,128)(2,1)S(1)}, u32[]{:S(2)}, u32[]{:S(2)}) collective-permute-start(bf16[1,256,512]{2,1,0:T(8,128)(2,1)S(1)} %copy-done.1), channel_id=1, source_target_pairs={{0,8},{8,0},{1,9},{9,1},{2,10},{10,2},{3,11},{11,3},{4,12},{12,4},... | collective-permute-start | bytes 786440 | tf_op jit(solution)/shard_map/ppermute | solution.py:256
  31.6 15.1 %collective-permute-start.6 = (bf16[128,512]{1,0:T(8,128)(2,1)S(1)}, bf16[128,512]{1,0:T(8,128)(2,1)S(1)}, u32[]{:S(2)}, u32[]{:S(2)}) collective-permute-start(bf16[128,512]{1,0:T(8,128)(2,1)S(1)} %shard_map.100.refs_1_), channel_id=1, source_target_pairs={{0,16},{16,32},{32,48},{48,64},{64,80},{80,96},{96,112},{112,0},{1... | collective-permute-start | bytes 393224 | tf_op jit(solution)/shard_map/ppermute | solution.py:256
  33.6 13.1 %collective-permute-start.7 = (bf16[128,512]{1,0:T(8,128)(2,1)S(1)}, bf16[128,512]{1,0:T(8,128)(2,1)S(1)}, u32[]{:S(2)}, u32[]{:S(2)}) collective-permute-start(bf16[128,512]{1,0:T(8,128)(2,1)S(1)} %shard_map.100.refs_1_), channel_id=1, source_target_pairs={{0,112},{16,0},{32,16},{48,32},{64,48},{80,64},{96,80},{112,96},{1... | collective-permute-start | bytes 393224 | tf_op jit(solution)/shard_map/ppermute | solution.py:256
  46.7 15.4 %copy-start.4 = (bf16[512]{0:T(512)(128)(2,1)S(1)}, bf16[512]{0:T(512)(128)(2,1)}, u32[]{:S(2)}) copy-start(bf16[512]{0:T(512)(128)(2,1)} %param.13) | copy-start | bytes 3076
  46.7 15.4 %copy-start.2 = (s32[32,256]{1,0:T(8,128)S(1)}, s32[32,256]{1,0:T(8,128)}, u32[]{:S(2)}) copy-start(s32[32,256]{1,0:T(8,128)} %refs_2_.3) | copy-start | bytes 98308
  46.7 15.4 %copy-start.3 = (s32[32]{0:T(128)S(1)}, s32[32]{0:T(128)}, u32[]{:S(2)}) copy-start(s32[32]{0:T(128)} %refs_1_.5) | copy-start | bytes 388
  46.8 22.0 %copy-start = (bf16[1,1024,512]{2,1,0:T(8,128)(2,1)S(1)}, bf16[1,1024,512]{2,1,0:T(8,128)(2,1)}, u32[]{:S(2)}) copy-start(bf16[1,1024,512]{2,1,0:T(8,128)(2,1)} %refs_1_.7) | copy-start | bytes 3145732
  46.8 11.9 %collective-permute-start.8 = (bf16[128,512]{1,0:T(8,128)(2,1)S(1)}, bf16[128,512]{1,0:T(8,128)(2,1)S(1)}, u32[]{:S(2)}, u32[]{:S(2)}) collective-permute-start(bf16[128,512]{1,0:T(8,128)(2,1)S(1)} %shard_map.101.refs_1_), channel_id=1, source_target_pairs={{0,48},{16,64},{32,80},{48,96},{64,112},{80,0},{96,16},{112,32},{1... | collective-permute-start | bytes 393224 | tf_op jit(solution)/shard_map/ppermute | solution.py:256
  50.4 8.3 %collective-permute-start.9 = (bf16[128,512]{1,0:T(8,128)(2,1)S(1)}, bf16[128,512]{1,0:T(8,128)(2,1)S(1)}, u32[]{:S(2)}, u32[]{:S(2)}) collective-permute-start(bf16[128,512]{1,0:T(8,128)(2,1)S(1)} %shard_map.101.refs_1_), channel_id=1, source_target_pairs={{0,96},{16,112},{32,0},{48,16},{64,32},{80,48},{96,64},{112,80},{1... | collective-permute-start | bytes 393224 | tf_op jit(solution)/shard_map/ppermute | solution.py:256
  58.7 4.2 %collective-permute-start.10 = (bf16[128,512]{1,0:T(8,128)(2,1)S(1)}, bf16[128,512]{1,0:T(8,128)(2,1)S(1)}, u32[]{:S(2)}, u32[]{:S(2)}) collective-permute-start(bf16[128,512]{1,0:T(8,128)(2,1)S(1)} %shard_map.102.refs_2_), channel_id=1, source_target_pairs={{0,8},{8,0},{1,9},{9,1},{2,10},{10,2},{3,11},{11,3},{4,12},{12,4},... | collective-permute-start | bytes 393224 | tf_op jit(solution)/shard_map/ppermute | solution.py:256
  58.8 8.0 %collective-permute-start.11 = (bf16[128,512]{1,0:T(8,128)(2,1)S(1)}, bf16[128,512]{1,0:T(8,128)(2,1)S(1)}, u32[]{:S(2)}, u32[]{:S(2)}) collective-permute-start(bf16[128,512]{1,0:T(8,128)(2,1)S(1)} %shard_map.102.refs_2_), channel_id=1, source_target_pairs={{0,128},{128,0},{1,129},{129,1},{2,130},{130,2},{3,131},{131,3},{4... | collective-permute-start | bytes 393224 | tf_op jit(solution)/shard_map/ppermute | solution.py:256
  61.0 7.4 %collective-permute-start.12 = (bf16[128,512]{1,0:T(8,128)(2,1)S(1)}, bf16[128,512]{1,0:T(8,128)(2,1)S(1)}, u32[]{:S(2)}, u32[]{:S(2)}) collective-permute-start(bf16[128,512]{1,0:T(8,128)(2,1)S(1)} %shard_map.102.refs_2_), channel_id=1, source_target_pairs={{0,136},{8,128},{128,8},{136,0},{1,137},{9,129},{129,9},{137,1},{2... | collective-permute-start | bytes 393224 | tf_op jit(solution)/shard_map/ppermute | solution.py:287
